TPU v7x, 128 devices: a whole 4x4x4 slice. The times are simulated.
128 devices in a mesh: dp: 1, etp: 64 (over z, y, x), ep: 2 (over core).
Axes of the slice: x: 4, y: 4, z: 4, core: 2. Of those that a mesh axis runs over, the one named last changes fastest.
Arguments:
- hidden: bfloat16 [8192, 1536], P(('dp', 'ep'))
- expert_ids: int32 [8192, 8], P(('dp', 'ep'))
- gate_wts: float32 [8192, 8], P(('dp', 'ep'))
- slot_pos: int32 [8192, 8], P(('dp', 'ep'))
- w_gate: bfloat16 [40, 1536, 512], P('ep', None, 'etp')
- w_up: bfloat16 [40, 1536, 512], P('ep', None, 'etp')
- w_down: bfloat16 [40, 512, 1536], P('ep', 'etp')
Outputs:
- output: bfloat16 [8192, 1536], P(('dp', 'ep'))
All inputs are finite; a program needn't handle non-finite values.
Results may differ from a plain program's by a relative error of at most 0.001.
Values are sent between devices in bfloat16 or wider.
A program may use at most 1 GiB of HBM per device.

v0:
```python
import jax
import jax.numpy as jnp
from jax import lax
from jax.sharding import PartitionSpec as P


def solution(mesh):
    group = mesh.shape['ep']
    row_spec = P(('dp', 'ep'), None)
    col_spec = P('ep', None, 'etp')
    in_specs = (row_spec, row_spec, row_spec, row_spec, col_spec, col_spec, P('ep', 'etp', None))

    def device_step(hidden, expert_ids, gate_wts, slot_pos, w_gate, w_up, w_down):
        rows_dev, d_model = hidden.shape
        top_k = expert_ids.shape[1]
        local_experts = w_gate.shape[0]
        experts = local_experts * group
        local_cap = ((5 * top_k * rows_dev) // (4 * experts) + 7) // 8 * 8
        capacity = group * local_cap
        tokens = rows_dev * group
        n_slots = local_experts * capacity
        all_hidden = lax.all_gather(hidden, 'ep', axis=0, tiled=True)
        all_ids = lax.all_gather(expert_ids, 'ep', axis=0, tiled=True)
        all_gates = lax.all_gather(gate_wts, 'ep', axis=0, tiled=True)
        all_pos = lax.all_gather(slot_pos, 'ep', axis=0, tiled=True)
        local_ids = all_ids - lax.axis_index('ep') * local_experts
        is_kept = (all_pos >= 0) & (local_ids >= 0) & (local_ids < local_experts)
        slot_index = jnp.where(is_kept, local_ids * capacity + all_pos, n_slots).reshape(-1)
        token_index = jnp.broadcast_to(jnp.arange(tokens, dtype=jnp.int32)[:, None], (tokens, top_k)).reshape(-1)
        slot_token = jnp.full((n_slots,), tokens, jnp.int32).at[slot_index].set(token_index, mode='drop')
        slot_gate = jnp.zeros((n_slots,), jnp.float32).at[slot_index].set(all_gates.reshape(-1), mode='drop')
        buffer = jnp.take(all_hidden, slot_token, axis=0, mode='fill', fill_value=0).reshape(local_experts, capacity, d_model)
        h_gate = jnp.einsum('ecd,edf->ecf', buffer, w_gate, preferred_element_type=jnp.float32)
        h_up = jnp.einsum('ecd,edf->ecf', buffer, w_up, preferred_element_type=jnp.float32)
        hidden_act = (jax.nn.silu(h_gate) * h_up).astype(jnp.bfloat16)
        expert_out = jnp.einsum('ecf,efd->ecd', hidden_act, w_down, preferred_element_type=jnp.float32)
        weighted = expert_out.reshape(n_slots, d_model) * slot_gate[:, None]
        part_sum = jax.ops.segment_sum(weighted, slot_token, num_segments=tokens)
        own_rows = lax.psum_scatter(part_sum, 'ep', scatter_dimension=0, tiled=True)
        summed = lax.psum(own_rows, 'etp')
        return summed.astype(jnp.bfloat16)

    return jax.shard_map(device_step, mesh=mesh, in_specs=in_specs, out_specs=row_spec, check_vma=False)
```

profile of v0, /device:TPU:0, one launch (start us, length us, event | category | flops | bytes accessed | tf_op | source)
XLA Modules:
  0.0 2135.4 jit_solution(898849497398860719)
XLA Ops:
  6.5 0.0 copy-start
  6.5 0.0 all-gather.2.cloned.1.call-start
  6.5 0.7 all-gather.2.cloned.1.call-update
  7.3 0.0 reduce-scatter.5.cloned.1.call-start
  7.3 2.0 all_gather.13
  9.3 2.0 all_gather.12
  11.3 0.1 add_select_fusion
  11.4 2.7 copy.10
  14.0 4.4 reshape.53
  18.4 2.0 all_gather.15
  20.4 2.7 copy.11
  23.1 3.6 reshape.77
  26.7 2.3 broadcast_in_dim.42
  29.0 3.6 reshape.69
  32.6 0.3 compare_select_fusion
  32.9 239.7 %scatter_custom_fusion = s32[40960]{0:T(1024)S(1)} fusion(s32[65536]{0:T(1024)S(1)} %bitcast.13, s32[65536]{0:T(1024)S(1)} %reshape.69, s32[]{:T(128)} %constant.11.clone.1), kind=kCustom, calls=%fused_computation.28 | custom fusion | bytes 163844 | tf_op jit(solution)/shard_map/scatter | solution.py:30
  272.6 0.0 copy-start.2
  272.6 0.1 compare_and_fusion
  272.7 0.7 broadcast_in_dim.44
  273.4 240.2 %scatter_custom_fusion.1 = f32[40960]{0:T(1024)} fusion(s32[65536]{0:T(1024)S(1)} %bitcast.14, f32[65536]{0:T(1024)S(1)} %reshape.77, f32[]{:T(128)} %constant.10.clone.1), kind=kCustom, calls=%fused_computation.26 | custom fusion | bytes 163844 | tf_op jit(solution)/shard_map/scatter | solution.py:31
  513.6 0.0 copy-done.2
  513.7 0.0 all-gather.2.cloned.1.call-done
  513.7 0.0 copy-start.1
  513.7 0.0 copy-start.5
  513.7 253.0 %gather_fusion = bf16[40960,1536]{1,0:T(8,128)(2,1)} fusion(bf16[8192,1536]{1,0:T(8,128)(2,1)} %all-gather.2.cloned.1.call-done, s32[40960]{0:T(1024)S(1)} %fusion.15), kind=kCustom, calls=%fused_computation | custom fusion | bytes 251822080 | tf_op jit(solution)/shard_map/jit(_take)/gather | solution.py:32
  766.7 0.0 copy-done.1
  766.7 0.0 copy-done.5
  766.8 0.0 copy-start.4
  766.8 39.8 %fusion.1 = f32[20,2048,8]{1,2,0:T(8,128)S(1)} fusion(bf16[20,1536,8]{1,2,0:T(8,128)(2,1)S(1)} %copy-done.5, bf16[20,2048,1536]{2,1,0:T(8,128)(2,1)} %bitcast.1, pred[20,2048]{1,0:T(8,128)(4,1)S(1)} %copy-done.1), kind=kOutput, calls=%fused_computation.7 | convolution fusion | flops 1069547520 | bytes 127672320 | tf_op jit(solution)/shard_map/ecd,edf->ecf/dot_general | solution.py:33
  806.6 0.0 copy-done
  806.6 0.0 copy-done.4
  806.6 0.0 copy-start.3
  806.6 129.0 %fusion.8 = f32[20,2048,1536]{2,1,0:T(8,128)} fusion(bf16[20,8,1536]{2,1,0:T(8,128)(2,1)S(1)} %copy-done, bf16[20,1536,8]{1,2,0:T(8,128)(2,1)S(1)} %copy-done.4, bf16[20,2048,1536]{2,1,0:T(8,128)(2,1)} %bitcast.1, pred[20,2048]{1,0:T(8,128)(4,1)S(1)} %copy-done.1, f32[20,2048,8]{1,2,0:T(8,128)S(1)} %fusion.1), kind=kOutput, calls=%fused_computation.14 | convolution fusion | flops 2078146560 | bytes 379822080 | tf_op jit(solution)/shard_map/ecf,efd->ecd/dot_general | solution.py:36
  935.6 0.0 copy-done.3
  935.6 160.9 %bitcast_multiply_fusion = f32[40960,1536]{1,0:T(8,128)} fusion(f32[20,2048,1536]{2,1,0:T(8,128)} %fusion.8, f32[40960]{0:T(1024)S(1)} %copy-done.3), kind=kLoop, calls=%fused_computation.4 | loop fusion | flops 62914560 | bytes 503480320 | tf_op jit(solution)/shard_map/mul | solution.py:37
  1096.6 412.0 %scatter_custom_fusion.2 = f32[8192,1536]{1,0:T(8,128)} fusion(s32[40960]{0:T(1024)} %copy-done.2, f32[40960,1536]{1,0:T(8,128)} %bitcast_multiply_fusion, f32[]{:T(128)} %constant.10.clone.1), kind=kCustom, calls=%fused_computation.10 | custom fusion | flops 62914560 | bytes 50332160 | tf_op jit(solution)/shard_map/scatter-add | solution.py:38
  1508.5 0.0 reduce-scatter.5.cloned.1.call-update
  1508.6 57.1 %reduce-scatter.5.cloned.1.call-done = f32[4096,1536]{1,0:T(8,128)} async-done(((f32[8192,1536]{1,0:T(8,128)}), f32[4096,1536]{1,0:T(8,128)}) %reduce-scatter.5.cloned.1.call-update) | async-done | bytes 25165840
  1565.7 562.9 %all-reduce.2 = bf16[4096,1536]{1,0:T(8,128)(2,1)} all-reduce(f32[4096,1536]{1,0:T(8,128)} %reduce-scatter.5.cloned.1.call-done), channel_id=1, replica_groups=mesh['dp'=1,'etp'=64,'ep'=2] {'etp'}, use_global_device_ids=true, to_apply=%region_4.5 | all-reduce | flops 6291456 | bytes 37748736 | tf_op jit(solution)/shard_map/psum | solution.py:40
  (1 shorter events, 0.0 us)
Async XLA Ops:
  6.5 800.1 %copy-start = (bf16[20,8,1536]{2,1,0:T(8,128)(2,1)S(1)}, bf16[20,8,1536]{2,1,0:T(8,128)(2,1)}, u32[]{:S(2)}) copy-start(bf16[20,8,1536]{2,1,0:T(8,128)(2,1)} %param.13) | copy-start | bytes 1474564
  6.5 507.1 %all-gather.2.cloned.1.call-start = ((), (), s32[]{:S(2)}) async-start(), calls=%async_computation.1 | async-start | bytes 37748736 | tf_op jit(solution)/shard_map/all_gather | solution.py:22
  7.3 1558.4 %reduce-scatter.5.cloned.1.call-start = ((), (), s32[]{:S(2)}) async-start(), calls=%async_computation.2 | async-start | bytes 75497472
  272.6 241.0 %copy-start.2 = (s32[40960]{0:T(1024)}, s32[40960]{0:T(1024)S(1)}, u32[]{:S(2)}) copy-start(s32[40960]{0:T(1024)S(1)} %scatter_custom_fusion) | copy-start | bytes 491524
  513.7 253.1 %copy-start.1 = (pred[20,2048]{1,0:T(8,128)(4,1)S(1)}, pred[20,2048]{1,0:T(8,128)(4,1)}, u32[]{:S(2)}) copy-start(pred[20,2048]{1,0:T(8,128)(4,1)} %broadcast_in_dim.44) | copy-start | bytes 122884
  513.7 253.1 %copy-start.5 = (bf16[20,1536,8]{1,2,0:T(8,128)(2,1)S(1)}, bf16[20,1536,8]{1,2,0:T(8,128)(2,1)}, u32[]{:S(2)}) copy-start(bf16[20,1536,8]{1,2,0:T(8,128)(2,1)} %param.11) | copy-start | bytes 1474564
  766.8 39.9 %copy-start.4 = (bf16[20,1536,8]{1,2,0:T(8,128)(2,1)S(1)}, bf16[20,1536,8]{1,2,0:T(8,128)(2,1)}, u32[]{:S(2)}) copy-start(bf16[20,1536,8]{1,2,0:T(8,128)(2,1)} %param.12) | copy-start | bytes 1474564
  806.6 129.0 %copy-start.3 = (f32[40960]{0:T(1024)S(1)}, f32[40960]{0:T(1024)}, u32[]{:S(2)}) copy-start(f32[40960]{0:T(1024)} %scatter_custom_fusion.1) | copy-start | bytes 491524
Sparse Core Ops, SparseCore 0:
  9.0 45.5 all-gather.1
  1508.7 56.9 reduce-scatter.4
where the time goes:
time: 2140 us
  local copies, waits for them, and re-layouts  753 us (35%)
  other arithmetic  573 us (27%)
  blocking collectives  569 us (27%)
  matrix products  169 us (8%)
  waiting for transfers between devices  57.9 us (3%)
    psum x1, blocking collectives, device_step(): summed = lax.psum(own_rows, 'etp')  563 us
    scatter-add x1, other arithmetic, device_step(): part_sum = jax.ops.segment_sum(weighted, slot_token, num_segments=tokens)  412 us
    gather x1, local copies, waits for them, and re-layouts, device_step(): jnp.take(all_hidden, slot_token, axis=0, mode='fill', fill_value=0)  253 us
    scatter x1, local copies, waits for them, and re-layouts, device_step(): jnp.zeros((n_slots,), jnp.float32).at[slot_index]  240 us
    scatter x1, local copies, waits for them, and re-layouts, device_step(): jnp.full((n_slots,), tokens, jnp.int32).at[slot_index]  240 us
    mul x1, other arithmetic, device_step(): weighted = expert_out.reshape(n_slots, d_model) * slot_gate[:, None]  161 us
    dot_general x1, matrix products, device_step(): jnp.einsum('ecf,efd->ecd', hidden_act, w_down, preferred_element_type=jnp...  129 us
    unnamed x3, waiting for transfers between devices  57.8 us
  transfers between devices with their start and end apart: 2, of which 1 were waited for; matrix products, arithmetic and copies ran while one was open for 23% of the time, Pallas kernels for 0%

commit v1 on v0

v1 whole, which is shorter than its diff:
```python
import jax
import jax.numpy as jnp
from jax import lax
from jax.sharding import PartitionSpec as P


def split3(a):
    hi = lax.reduce_precision(a, 8, 7)
    rest = a - hi
    mid = lax.reduce_precision(rest, 8, 7)
    low = rest - mid
    return [v.astype(jnp.bfloat16) for v in (hi, mid, low)]


def solution(mesh):
    row_spec = P(('dp', 'ep'), None)
    col_spec = P('ep', None, 'etp')
    in_specs = (row_spec, row_spec, row_spec, row_spec, col_spec, col_spec, P('ep', 'etp', None))

    def device_step(hidden, expert_ids, gate_wts, slot_pos, w_gate, w_up, w_down):
        rows, d_model = hidden.shape
        top_k = expert_ids.shape[1]
        width = w_gate.shape[2]
        w_gate = lax.all_gather(w_gate, 'ep', axis=0, tiled=True)
        w_up = lax.all_gather(w_up, 'ep', axis=0, tiled=True)
        w_down = lax.all_gather(w_down, 'ep', axis=0, tiled=True)
        experts = w_gate.shape[0]
        cols = experts * width
        wg = w_gate.transpose(1, 0, 2).reshape(d_model, cols)
        wu = w_up.transpose(1, 0, 2).reshape(d_model, cols)
        wd = w_down.reshape(cols, d_model)
        kept = slot_pos >= 0
        top = jnp.max(jnp.where(kept, gate_wts, 0.0), axis=1, keepdims=True)
        top = jnp.where(top > 0, top, 1.0)
        rel = gate_wts / top
        col_expert = jnp.arange(cols, dtype=jnp.int32) // width
        gate = jnp.zeros((rows, cols), jnp.float32)
        for j in range(top_k):
            hit = (expert_ids[:, j:j + 1] == col_expert[None, :]) & kept[:, j:j + 1]
            gate = jnp.where(hit, rel[:, j:j + 1], gate)
        h_gate = jnp.dot(hidden, wg, preferred_element_type=jnp.float32)
        h_up = jnp.dot(hidden, wu, preferred_element_type=jnp.float32)
        act = lax.reduce_precision(jax.nn.silu(h_gate) * h_up, 8, 7)
        scaled = jnp.where(gate > 0, act * gate, 0.0)
        parts = jnp.concatenate(split3(scaled), axis=1)
        part_sum = jnp.dot(parts, jnp.concatenate([wd] * 3, axis=0), preferred_element_type=jnp.float32)
        own = lax.psum_scatter(part_sum, 'etp', scatter_dimension=0, tiled=True)
        n_own = own.shape[0]
        own_top = lax.dynamic_slice_in_dim(top, lax.axis_index('etp') * n_own, n_own, 0)
        own = (own * own_top).astype(jnp.bfloat16)
        return lax.all_gather(own, 'etp', axis=0, tiled=True)

    return jax.shard_map(device_step, mesh=mesh, in_specs=in_specs, out_specs=row_spec, check_vma=False)
```

time: 2140 us -> 422 us (0.20)
  local copies, waits for them, and re-layouts: 753 us -> 12.5 us
  other arithmetic: 573 us -> 3.8 us
  blocking collectives: 569 us -> 7.64 us
  waiting for transfers between devices: 57.9 us -> 341 us
  matrix products: 169 us -> 42.3 us
    psum x1 -> x0, blocking collectives: 563 us -> none  [device_step(): summed = lax.psum(own_rows, 'etp')]
    scatter x2 -> x0, local copies, waits for them, and re-layouts: 480 us -> none  [the longest x1 240 us: device_step(): jnp.zeros((n_slots,), jnp.float32).at[slot_index]]
    scatter-add x1 -> x0, other arithmetic: 412 us -> none  [device_step(): part_sum = jax.ops.segment_sum(weighted, slot_token, num_segments=tokens)]
    gather x1 -> x0, local copies, waits for them, and re-layouts: 253 us -> none  [device_step(): jnp.take(all_hidden, slot_token, axis=0, mode='fill', fill_value=0)]
    reduce_scatter x0 -> x1, waiting for transfers between devices: none -> 252 us  [device_step(): own = lax.psum_scatter(part_sum, 'etp', scatter_dimension=0, tiled=True)]
    mul x1, other arithmetic: 161 us -> 0.08 us  [device_step(): own = (own * own_top).astype(jnp.bfloat16)]
    dot_general x2 -> x3, matrix products: 169 us -> 42.3 us  [the longest x1 20.1 us: device_step(): jnp.dot(parts, jnp.concatenate([wd] * 3, axis=0), preferred_element_type=...]
    all_gather x1, waiting for transfers between devices: 0.02 us -> 89.1 us  [device_step(): return lax.all_gather(own, 'etp', axis=0, tiled=True)]
  transfers between devices with their start and end apart: 2 -> 2, of which waited for: 1 -> 2; matrix products, arithmetic and copies ran while one was open for 23% -> 0% of each run, Pallas kernels for 0% -> 0%
where the time goes in v1:
time: 422 us; the launch traced here: 421 us
  waiting for transfers between devices  341 us (81%)
  matrix products  42.3 us (10%)
  between operations  13.5 us (3%)
  local copies, waits for them, and re-layouts  12.5 us (3%)
  blocking collectives  7.64 us (2%)
    reduce_scatter x1, waiting for transfers between devices, device_step(): own = lax.psum_scatter(part_sum, 'etp', scatter_dimension=0, tiled=True)  252 us
    all_gather x1, waiting for transfers between devices, device_step(): return lax.all_gather(own, 'etp', axis=0, tiled=True)  89.1 us
    dot_general x1, matrix products, device_step(): jnp.dot(parts, jnp.concatenate([wd] * 3, axis=0), preferred_element_type=...  20.1 us
    dot_general x1, matrix products, device_step(): h_up = jnp.dot(hidden, wu, preferred_element_type=jnp.float32)  14.8 us
    unnamed x7, local copies, waits for them, and re-layouts  10.5 us
  transfers between devices with their start and end apart: 2, of which 2 were waited for; matrix products, arithmetic and copies ran while one was open for 0% of the time, Pallas kernels for 0%

profile of v1, /device:TPU:0, one launch (start us, length us, event | category | flops | bytes accessed | tf_op | source)
XLA Modules:
  0.0 420.9 jit_solution(926265349814363335)
XLA Ops:
  6.5 0.0 reduce-scatter.2.cloned.1.call-start
  6.5 1.0 select_reduce_fusion
  7.6 0.4 slice_reduce_fusion.7
  7.9 0.9 broadcast_divide_fusion
  8.9 0.1 fusion.23
  9.0 1.6 fusion.22
  10.5 2.5 all_gather.12
  13.0 2.5 all_gather.13
  15.5 0.0 slice-start
  15.6 2.6 all_gather.14
  18.2 0.0 slice-start.1
  18.2 0.0 slice-start.2
  18.2 7.4 %fusion.15 = f32[4096,320]{0,1:T(8,128)S(1)} fusion(bf16[4096,1536]{1,0:T(8,128)(2,1)} %param.7, bf16[40,1536,8]{1,2,0:T(8,128)(2,1)S(1)} %all_gather.12), kind=kOutput, calls=%fused_computation.22 | convolution fusion | flops 4026531840 | bytes 18808832 | tf_op jit(solution)/shard_map/dot_general | solution.py:41
  25.6 0.0 slice-done
  25.6 0.0 slice-done.1
  25.6 0.0 slice-done.2
  25.6 14.8 %reduce-precision_convert_fusion.1 = (bf16[4096,320]{0,1:T(8,128)(2,1)}, bf16[4096,320]{0,1:T(8,128)(2,1)}, bf16[4096,320]{0,1:T(8,128)(2,1)}) fusion(bf16[4096,1536]{1,0:T(8,128)(2,1)S(1)} %bitcast.53, bf16[40,1536,8]{1,2,0:T(8,128)(2,1)S(1)} %all_gather.13, f32[4096,320]{0,1:T(8,128)S(1)} %fusion.15, f32[4096]{0:T(1024)S(1)} %bitcast.37, ...), kind=kOutput, calls=%fused_computation.9 | convolution fusion | flops 4078960640 | bytes 26969344 | tf_op jit(solution)/shard_map/dot_general | solution.py:42
  40.5 20.1 %fusion = f32[4096,1536]{1,0:T(8,128)} fusion(bf16[4096,320]{0,1:T(8,128)(2,1)} %get-tuple-element.16, bf16[4096,320]{0,1:T(8,128)(2,1)} %get-tuple-element.17, bf16[4096,320]{0,1:T(8,128)(2,1)} %get-tuple-element.15, bf16[320,1536]{1,0:T(8,128)(2,1)S(1)} %bitcast.34), kind=kOutput, calls=%fused_computation | convolution fusion | flops 12112035840 | bytes 34013184 | tf_op jit(solution)/shard_map/dot_general | solution.py:46
  60.6 0.0 reduce-scatter.2.cloned.1.call-update
  60.6 0.0 all-gather.2.cloned.1.call-start
  60.7 0.1 fusion.20
  60.7 251.9 %reduce-scatter.2.cloned.1.call-done = f32[64,1536]{1,0:T(8,128)} async-done(((f32[4096,1536]{1,0:T(8,128)}), f32[64,1536]{1,0:T(8,128)}) %reduce-scatter.2.cloned.1.call-update) | async-done | bytes 393232 | tf_op jit(solution)/shard_map/reduce_scatter | solution.py:47
  312.7 1.8 multiply_convert_fusion
  314.4 0.0 all-gather.2.cloned.1.call-update
  314.5 89.1 %all-gather.2.cloned.1.call-done = bf16[4096,1536]{1,0:T(8,128)(2,1)} async-done(((bf16[64,1536]{1,0:T(8,128)(2,1)}), bf16[4096,1536]{1,0:T(8,128)(2,1)}) %all-gather.2.cloned.1.call-update) | async-done | bytes 12582928 | tf_op jit(solution)/shard_map/all_gather | solution.py:51
  403.6 10.5 %copy.9 = bf16[4096,1536]{1,0:T(8,128)(2,1)} copy(bf16[4096,1536]{1,0:T(8,128)(2,1)} %all-gather.2.cloned.1.call-done) | data formatting | bytes 25165824
  (3 shorter events, 0.0 us)
Async XLA Ops:
  6.5 306.1 %reduce-scatter.2.cloned.1.call-start = ((), (), s32[]{:S(2)}) async-start(), calls=%async_computation.1 | async-start | bytes 25559040 | tf_op jit(solution)/shard_map/reduce_scatter | solution.py:47
  15.5 10.1 %slice-start = ((s8[12582912]{0:T(1024)(128)(4,1)}), s8[4194304]{0:T(1024)(128)(4,1)S(1)}, s32[]{:S(2)}) async-start(s8[12582912]{0:T(1024)(128)(4,1)} %bitcast.52), calls=%async_computation.3 | async-start | bytes 8388608
  18.2 7.4 %slice-start.1 = ((s8[12582912]{0:T(1024)(128)(4,1)}), s8[4194304]{0:T(1024)(128)(4,1)S(1)}, s32[]{:S(2)}) async-start(s8[12582912]{0:T(1024)(128)(4,1)} %bitcast.52), calls=%async_computation.4 | async-start | bytes 8388608
  18.2 7.4 %slice-start.2 = ((s8[12582912]{0:T(1024)(128)(4,1)}), s8[4194304]{0:T(1024)(128)(4,1)S(1)}, s32[]{:S(2)}) async-start(s8[12582912]{0:T(1024)(128)(4,1)} %bitcast.52), calls=%async_computation.5 | async-start | bytes 8388608
  60.6 343.0 %all-gather.2.cloned.1.call-start = ((), (), s32[]{:S(2)}) async-start(), calls=%async_computation.2 | async-start | bytes 12779520 | tf_op jit(solution)/shard_map/all_gather | solution.py:51
Sparse Core Ops, SparseCore 0:
  60.7 251.9 reduce-scatter.1
  315.4 88.1 all-gather.1

commit v2 on v1

v2 whole, which is shorter than its diff:
```python
import functools

import jax
import jax.numpy as jnp
from jax import lax
from jax.experimental import pallas as pl
from jax.experimental.pallas import tpu as pltpu
from jax.sharding import PartitionSpec as P

MESH = pl.DeviceIdType.MESH
SIDE = 4


def split3(a):
    hi = lax.reduce_precision(a, 8, 7)
    rest = a - hi
    mid = lax.reduce_precision(rest, 8, 7)
    low = rest - mid
    return [v.astype(jnp.bfloat16) for v in (hi, mid, low)]


def coords():
    chip = lax.axis_index('etp')
    return chip // (SIDE * SIDE), (chip // SIDE) % SIDE, chip % SIDE


def chip_id(z, y, x):
    return {'etp': ((z % SIDE) * SIDE + y % SIDE) * SIDE + x % SIDE}


def greet(partners):
    barrier = pltpu.get_barrier_semaphore()
    for device_id in partners:
        pl.semaphore_signal(barrier, inc=1, device_id=device_id, device_id_type=MESH)
    pl.semaphore_wait(barrier, len(partners))


def push(src, dst, sems, n, device_id):
    send_sem, recv_sem = sems
    copy = pltpu.make_async_remote_copy(src_ref=src, dst_ref=dst, send_sem=send_sem.at[n], recv_sem=recv_sem.at[n],
                                        device_id=device_id, device_id_type=MESH)
    copy.start()
    return copy


def weight_kernel(w_ref, out_ref, ring_send, ring_recv, core_send, core_recv, own_sem):
    z, y, x = coords()
    core = lax.axis_index('ep')
    other = {'ep': 1 - core}
    rows = w_ref.shape[1] // 2
    half = w_ref.shape[2] // 2
    rings = (ring_send, ring_recv)
    cores = (core_send, core_recv)
    right = (chip_id(z, y, x + 1), chip_id(z, y + 1, x))
    left = (chip_id(z, y, x + 3), chip_id(z, y + 3, x))
    place = (x, y)
    greet(list(right) + list(left) + [other])

    def src(d, h):
        return w_ref.at[:, pl.ds(d * rows, rows), pl.ds(h * half, half)]

    def box(d, i, h, c):
        return out_ref.at[:, d, i % SIDE, c, :, pl.ds(h * half, half)]

    flights = []
    firsts = []
    for d in range(2):
        me = place[d]
        firsts.append((push(src(d, 0), box(d, me, 0, core), rings, 6 * d, right[d]),
                       push(src(d, 1), box(d, me, 1, core), rings, 6 * d + 1, left[d])))
    seconds = []
    for d in range(2):
        me = place[d]
        seconds.append((push(src(d, 1), box(d, me, 1, core), rings, 6 * d + 2, right[d]),
                        push(src(d, 0), box(d, me, 0, core), rings, 6 * d + 3, left[d])))
        for h in range(2):
            flights.append(push(src(d, h), box(d, me, h, core), cores, 8 * d + h, other))
    owns = []
    for d in range(2):
        own = pltpu.make_async_copy(w_ref.at[:, pl.ds(d * rows, rows), :], out_ref.at[:, d, place[d], core], own_sem.at[d])
        own.start()
        owns.append(own)
    thirds = []
    for d in range(2):
        me = place[d]
        from_left, from_right = box(d, me + 3, 0, core), box(d, me + 1, 1, core)
        firsts[d][0].wait_recv()
        one = push(from_left, from_left, rings, 6 * d + 4, right[d])
        flights.append(push(from_left, from_left, cores, 8 * d + 2, other))
        firsts[d][1].wait_recv()
        two = push(from_right, from_right, rings, 6 * d + 5, left[d])
        flights.append(push(from_right, from_right, cores, 8 * d + 3, other))
        thirds.append((one, two))
    for d in range(2):
        me = place[d]
        for n, (copy, i, h) in enumerate(((seconds[d][0], me + 3, 1), (seconds[d][1], me + 1, 0),
                                          (thirds[d][0], me + 2, 0), (thirds[d][1], me + 2, 1))):
            copy.wait_recv()
            flights.append(push(box(d, i, h, core), box(d, i, h, core), cores, 8 * d + 4 + n, other))
    for copy in flights:
        copy.wait_recv()
    for pair in firsts + seconds + thirds:
        for copy in pair:
            copy.wait_send()
    for copy in flights:
        copy.wait_send()
    for own in owns:
        own.wait()


def gather_weights(weights):
    mats, rows, depth = weights.shape
    return pl.pallas_call(
        weight_kernel,
        out_shape=jax.ShapeDtypeStruct((mats, 2, SIDE, 2, rows // 2, depth), weights.dtype),
        in_specs=[pl.BlockSpec(memory_space=pltpu.VMEM)],
        out_specs=pl.BlockSpec(memory_space=pl.ANY),
        scratch_shapes=[pltpu.SemaphoreType.DMA((12,)), pltpu.SemaphoreType.DMA((12,)),
                        pltpu.SemaphoreType.DMA((16,)), pltpu.SemaphoreType.DMA((16,)),
                        pltpu.SemaphoreType.DMA((2,))],
        compiler_params=pltpu.CompilerParams(collective_id=0, has_side_effects=True),
        name='gather_weights',
    )(weights)


def combine_kernel(part_a, part_b, top_ref, out_ref, opp1, fin1, sum1, opp2, fin2, gath,
                   rs_send, rs_recv, ag_send, ag_recv, out_sem):
    z, y, x = coords()
    width = part_a.shape[3]
    n_rows = part_a.shape[2]
    third = out_ref.shape[4] // 3
    ups = {'z': chip_id(z + 1, y, x), 'y': chip_id(z, y + 1, x), 'x': chip_id(z, y, x + 1), 'd': chip_id(z, y + 3, x + 1)}
    downs = {'z': chip_id(z + 3, y, x), 'y': chip_id(z, y + 3, x), 'x': chip_id(z, y, x + 3), 'd': chip_id(z, y + 1, x + 3)}
    greet(list(ups.values()) + list(downs.values()))
    sems = (rs_send, rs_recv)
    started = []

    def ring_sum(base, ring, me, block, half, opp, fin):
        right, left = ups[ring], downs[ring]
        o, r, l = (me + 2) % SIDE, (me + 1) % SIDE, (me + 3) % SIDE
        one = push(half(block(o), 0), opp.at[0], sems, base, right)
        two = push(half(block(o), 1), opp.at[1], sems, base + 1, left)
        three = push(half(block(r), 1), half(fin.at[0], 1), sems, base + 2, right)
        four = push(half(block(l), 0), half(fin.at[1], 0), sems, base + 3, left)

        def forward():
            one.wait_recv()
            opp[0] = opp[0] + half(block(r), 0)[...]
            five = push(opp.at[0], half(fin.at[0], 0), sems, base + 4, right)
            two.wait_recv()
            opp[1] = opp[1] + half(block(l), 1)[...]
            six = push(opp.at[1], half(fin.at[1], 1), sems, base + 5, left)
            started.extend((one, two, three, four, five, six))

            def finish():
                for copy in (three, four, five, six):
                    copy.wait_recv()
                return block(me)[...] + fin[0] + fin[1]
            return finish
        return forward

    two_blocks = lambda ref, h: ref.at[pl.ds(2 * h, 2)]
    rows_half = lambda ref, h: ref.at[pl.ds(h * (n_rows // 2), n_rows // 2)]
    fwd_a = ring_sum(0, 'z', z, lambda i: part_a.at[i], two_blocks, opp1.at[0], fin1.at[0])
    fwd_b = ring_sum(6, 'd', x, lambda i: part_b.at[:, i], two_blocks, opp1.at[1], fin1.at[1])
    end_a, end_b = fwd_a(), fwd_b()
    sum1[0] = end_a()
    fwd_a = ring_sum(12, 'd', x, lambda i: sum1.at[0, i], rows_half, opp2.at[0], fin2.at[0])
    sum1[1] = end_b()
    fwd_b = ring_sum(18, 'z', z, lambda i: sum1.at[1, i], rows_half, opp2.at[1], fin2.at[1])
    end_a, end_b = fwd_a(), fwd_b()
    mine = jnp.concatenate([end_a(), end_b()], axis=1) * top_ref[...]
    mine = mine.astype(out_ref.dtype)
    for k in range(3):
        gath[k, z, y, x] = mine[:, k * third:(k + 1) * third]

    sems_ag = (ag_send, ag_recv)
    where = {'z': z, 'y': y, 'x': x}
    orders = ('xyz', 'yzx', 'zxy')

    def region(k, done, dim, i, h):
        index = []
        for name in 'zyx':
            if name == dim:
                index.append(i % SIDE)
            elif name in done:
                index.append(slice(None))
            else:
                index.append(where[name])
        return gath.at[(k, *index, pl.ds(h * (n_rows // 2), n_rows // 2))]

    for phase in range(3):
        firsts, seconds, thirds = [], [], []
        for k, order in enumerate(orders):
            dim, done = order[phase], order[:phase]
            spot = functools.partial(region, k, done, dim)
            me, base = where[dim], 18 * phase + 6 * k
            firsts.append((push(spot(me, 0), spot(me, 0), sems_ag, base, ups[dim]),
                           push(spot(me, 1), spot(me, 1), sems_ag, base + 1, downs[dim])))
        for k, order in enumerate(orders):
            dim, done = order[phase], order[:phase]
            spot = functools.partial(region, k, done, dim)
            me, base = where[dim], 18 * phase + 6 * k
            seconds.append((push(spot(me, 1), spot(me, 1), sems_ag, base + 2, ups[dim]),
                            push(spot(me, 0), spot(me, 0), sems_ag, base + 3, downs[dim])))
        for k, order in enumerate(orders):
            dim, done = order[phase], order[:phase]
            spot = functools.partial(region, k, done, dim)
            me, base = where[dim], 18 * phase + 6 * k
            firsts[k][0].wait_recv()
            one = push(spot(me + 3, 0), spot(me + 3, 0), sems_ag, base + 4, ups[dim])
            firsts[k][1].wait_recv()
            two = push(spot(me + 1, 1), spot(me + 1, 1), sems_ag, base + 5, downs[dim])
            thirds.append((one, two))
        for pair in seconds + thirds:
            for copy in pair:
                copy.wait_recv()
        for pair in firsts + seconds + thirds:
            started.extend(pair)
    lasts = []
    for k in range(3):
        last = pltpu.make_async_copy(gath.at[k], out_ref.at[:, :, :, :, pl.ds(k * third, third)], out_sem.at[k])
        last.start()
        lasts.append(last)
    for copy in started:
        copy.wait_send()
    for last in lasts:
        last.wait()


def combine(part_a, part_b, top):
    n_rows, width = part_a.shape[2:]
    blocks = (SIDE, SIDE, SIDE, n_rows)
    f32 = jnp.float32
    return pl.pallas_call(
        combine_kernel,
        out_shape=jax.ShapeDtypeStruct((*blocks, 2 * width), jnp.bfloat16),
        in_specs=[pl.BlockSpec(memory_space=pltpu.VMEM)] * 3,
        out_specs=pl.BlockSpec(memory_space=pl.ANY),
        scratch_shapes=[
            pltpu.VMEM((2, 2, 2, n_rows, width), f32),
            pltpu.VMEM((2, 2, SIDE, n_rows, width), f32),
            pltpu.VMEM((2, SIDE, n_rows, width), f32),
            pltpu.VMEM((2, 2, n_rows // 2, width), f32),
            pltpu.VMEM((2, 2, n_rows, width), f32),
            pltpu.VMEM((3, *blocks, 2 * width // 3), jnp.bfloat16),
            pltpu.SemaphoreType.DMA((24,)), pltpu.SemaphoreType.DMA((24,)),
            pltpu.SemaphoreType.DMA((54,)), pltpu.SemaphoreType.DMA((54,)),
            pltpu.SemaphoreType.DMA((3,)),
        ],
        compiler_params=pltpu.CompilerParams(collective_id=1, has_side_effects=True, vmem_limit_bytes=50 * 2 ** 20),
        name='combine',
    )(part_a, part_b, top)


def solution(mesh):
    row_spec = P(('dp', 'ep'), None)
    col_spec = P('ep', None, 'etp')
    in_specs = (row_spec, row_spec, row_spec, row_spec, col_spec, col_spec, P('ep', 'etp', None))

    def device_step(hidden, expert_ids, gate_wts, slot_pos, w_gate, w_up, w_down):
        rows, d_model = hidden.shape
        top_k = expert_ids.shape[1]
        local_experts, _, width = w_gate.shape
        z, y, x = coords()
        group = (x + y) % SIDE
        block = rows // SIDE ** 3

        def mine(a):
            a = a.reshape(SIDE, SIDE, SIDE, block, a.shape[1])
            picks = [lax.dynamic_index_in_dim(a[:, :, i], (group + SIDE - i) % SIDE, 1, keepdims=False) for i in range(SIDE)]
            return jnp.stack(picks, axis=1).reshape(SIDE * SIDE * block, a.shape[4])

        local = [w.transpose(0, 2, 1) for w in (w_gate, w_up)] + [w_down]
        local = jnp.stack([w.reshape(local_experts * width, d_model) for w in local])
        full = gather_weights(local)
        cols = 2 * SIDE * local_experts * width
        wg, wu, wd = full.reshape(3, cols, d_model)
        dim, place, core, expert, _ = jnp.unravel_index(jnp.arange(cols), (2, SIDE, 2, local_experts // 2, width))
        col_expert = (core * local_experts + dim * (local_experts // 2) + expert).astype(jnp.int32)

        hid, ids, gates, pos = mine(hidden), mine(expert_ids), mine(gate_wts), mine(slot_pos)
        kept = pos >= 0
        top = jnp.max(jnp.where(kept, gates, 0.0), axis=1, keepdims=True)
        top = jnp.where(top > 0, top, 1.0)
        rel = gates / top
        gate = jnp.zeros((hid.shape[0], cols), jnp.float32)
        for j in range(top_k):
            hit = (ids[:, j:j + 1] == col_expert[None, :]) & kept[:, j:j + 1]
            gate = jnp.where(hit, rel[:, j:j + 1], gate)
        nt = (((1,), (1,)), ((), ()))
        h_gate = lax.dot_general(hid, wg, nt, preferred_element_type=jnp.float32)
        h_up = lax.dot_general(hid, wu, nt, preferred_element_type=jnp.float32)
        act = lax.reduce_precision(jax.nn.silu(h_gate) * h_up, 8, 7)
        scaled = jnp.where(gate > 0, act * gate, 0.0)
        parts = jnp.concatenate(split3(scaled), axis=1)
        wd3 = jnp.concatenate([wd] * 3, axis=0)
        half = d_model // 2
        shape = (SIDE, SIDE, block, half)
        part_a = jnp.dot(parts, wd3[:, :half], preferred_element_type=jnp.float32).reshape(shape)
        part_b = jnp.dot(parts, wd3[:, half:], preferred_element_type=jnp.float32).reshape(shape)
        own_top = lax.dynamic_index_in_dim(top.reshape(SIDE * SIDE, block, 1), z * SIDE + x, 0, keepdims=False)
        return combine(part_a, part_b, own_top).reshape(rows, d_model)

    return jax.shard_map(device_step, mesh=mesh, in_specs=in_specs, out_specs=row_spec, check_vma=False)
```

time: 422 us -> 202 us (0.48)
  waiting for transfers between devices: 341 us -> 0 us
  Pallas kernels: 0 us -> 137 us
  local copies, waits for them, and re-layouts: 12.5 us -> 27.1 us
  between operations: 13.5 us -> 0.32 us
  matrix products: 42.3 us -> 34.1 us
  blocking collectives: 7.64 us -> 0 us
    reduce_scatter x1 -> x0, waiting for transfers between devices: 252 us -> none  [device_step(): own = lax.psum_scatter(part_sum, 'etp', scatter_dimension=0, tiled=True)]
    pallas_call x0 -> x2, Pallas kernels: none -> 137 us  [the longest x1 101 us: combine(): pl.pallas_call(combine_kernel, out_shape=jax.ShapeDtypeStruct((*blocks, 2...]
    all_gather x1 -> x0, waiting for transfers between devices: 89.1 us -> none  [device_step(): return lax.all_gather(own, 'etp', axis=0, tiled=True)]
    dot_general x3 -> x4, matrix products: 42.3 us -> 34.1 us  [the longest x1 13.9 us: device_step(): h_up = lax.dot_general(hid, wu, nt, preferred_element_type=jnp.float32)]
    all_gather x3 -> x0, blocking collectives: 7.64 us -> none  [the longest x1 2.63 us: device_step(): w_down = lax.all_gather(w_down, 'ep', axis=0, tiled=True)]
    another operation x0 -> x1, local copies, waits for them, and re-layouts: none -> 4.94 us  [device_step(): wg, wu, wd = full.reshape(3, cols, d_model)]
    unnamed x7 -> x9, local copies, waits for them, and re-layouts: 10.5 us -> 12 us
  transfers between devices with their start and end apart: 2 -> 0, of which waited for: 2 -> 0; matrix products, arithmetic and copies ran while one was open for 0% -> 0% of each run, Pallas kernels for 0% -> 0%
where the time goes in v2:
time: 202 us
  Pallas kernels  137 us (68%)
  matrix products  34.1 us (17%)
  local copies, waits for them, and re-layouts  27.1 us (13%)
  other arithmetic  3.07 us (2%)
    pallas_call x1, Pallas kernels, combine(): pl.pallas_call(combine_kernel, out_shape=jax.ShapeDtypeStruct((*blocks, 2...  101 us
    pallas_call x1, Pallas kernels, gather_weights(): pl.pallas_call(weight_kernel, out_shape=jax.ShapeDtypeStruct((mats, 2, SI...  35.9 us
    dot_general x1, matrix products, device_step(): h_up = lax.dot_general(hid, wu, nt, preferred_element_type=jnp.float32)  13.9 us
    unnamed x9, local copies, waits for them, and re-layouts  12 us
    dot_general x1, matrix products, device_step(): jnp.dot(parts, wd3[:, :half], preferred_element_type=jnp.float32)  7.99 us
    dot_general x1, matrix products, device_step(): jnp.dot(parts, wd3[:, half:], preferred_element_type=jnp.float32)  7.92 us
    slice x4, local copies, waits for them, and re-layouts, mine(): a[:, :, i]  5.79 us
    another operation x1, local copies, waits for them, and re-layouts, device_step(): wg, wu, wd = full.reshape(3, cols, d_model)  4.94 us

profile of v2, /device:TPU:0, one launch (start us, length us, event | category | flops | bytes accessed | tf_op | source)
XLA Modules:
  0.0 201.6 jit_solution(16956355420744768801)
XLA Ops:
  0.0 1.1 reshape.91
  1.1 0.2 fusion.35
  1.3 1.1 reshape.93
  2.4 0.2 fusion.37
  2.8 0.1 pad_add_fusion
  2.9 0.1 reshape.92
  3.0 1.1 reshape.94
  4.1 0.2 fusion.36
  4.4 0.2 select_reduce_fusion
  4.5 0.1 reshape.95
  4.7 0.1 reduce_max.14
  4.8 0.1 ge.12
  4.9 0.1 slice_reduce_fusion.7
  5.0 5.2 %fusion.33 = (bf16[4,4,1,64,1536]{4,3,2,1,0:T(8,128)(2,1)S(1)}, bf16[4,4,1,64,1536]{4,3,2,1,0:T(8,128)(2,1)S(1)}, bf16[4,4,1,64,1536]{4,3,2,1,0:T(8,128)(2,1)S(1)}, bf16[4,4,1,64,1536]{4,3,2,1,0:T(8,128)(2,1)S(1)}) fusion(bf16[4,4,4,64,1536]{4,3,2,1,0:T(8,128)(2,1)} %bitcast.93), kind=kLoop, calls=%fused_computation.98 | loop fusion | bytes 25165824 | tf_op jit(solution)/shard_map/slice | solution.py:271
  10.2 0.2 dynamic-slice_bitcast_fusion.2
  10.4 0.2 dynamic-slice_bitcast_fusion
  10.6 0.0 copy-start
  10.6 0.0 copy-start.1
  10.6 0.0 copy-start.2
  10.6 0.4 pad_maximum_fusion.4
  11.0 0.5 copy-done
  11.6 0.1 copy-done.1
  11.7 0.1 copy-done.2
  11.9 1.3 pad_maximum_fusion.5.w_ref
  13.2 35.9 %gather_weights.1 = bf16[3,2,4,2,80,1536]{5,4,3,2,1,0:T(8,128)(2,1)} custom-call(bf16[3,160,1536]{2,1,0:T(8,128)(2,1)} %pad_maximum_fusion.5.w_ref), custom_call_target="tpu_custom_call" | custom-call | tf_op jit(solution)/shard_map/gather_weights/pallas_call | solution.py:113
  49.0 4.9 %fusion.34 = (bf16[1,2,4,2,80,1536]{5,4,3,2,1,0:T(8,128)(2,1)S(1)}, bf16[1,2,4,2,80,1536]{5,4,3,2,1,0:T(8,128)(2,1)S(1)}, bf16[1,2,4,2,80,1536]{5,4,3,2,1,0:T(8,128)(2,1)S(1)}) fusion(bf16[3,2,4,2,80,1536]{5,4,3,2,1,0:T(8,128)(2,1)} %gather_weights.1), kind=kLoop, calls=%fused_computation.99 | loop fusion | bytes 23592960 | tf_op jit(solution)/shard_map/unstack | solution.py:278
  54.0 4.3 %fusion.40 = f32[1024,1280]{1,0:T(8,128)S(1)} fusion(bf16[1024,1536]{1,0:T(8,128)(2,1)S(1)} %bitcast.97, bf16[1280,1536]{1,0:T(8,128)(2,1)S(1)} %bitcast.95), kind=kOutput, calls=%fused_computation.105 | convolution fusion | flops 4026531840 | bytes 12320768 | tf_op jit(solution)/shard_map/dot_general | solution.py:292
  58.3 13.9 %reduce-precision_convert_fusion.1 = (bf16[1024,1280]{1,0:T(8,128)(2,1)S(1)}, bf16[1024,1280]{1,0:T(8,128)(2,1)S(1)}, bf16[1024,1280]{1,0:T(8,128)(2,1)}) fusion(bf16[1024,1536]{1,0:T(8,128)(2,1)S(1)} %bitcast.98, bf16[1280,1536]{1,0:T(8,128)(2,1)S(1)} %bitcast.94, f32[1024,1280]{1,0:T(8,128)S(1)} %fusion.40, f32[1024]{0:T(1024)S(1)} %bitcast.112, ...), kind=kOutput, calls=%fused_computation.5 | convolution fusion | flops 4078960640 | bytes 20263936 | tf_op jit(solution)/shard_map/dot_general | solution.py:293
  72.2 0.0 copy-start.3
  72.2 1.0 pad_maximum_fusion
  73.2 0.7 copy-done.3
  73.9 7.9 %fusion = f32[1024,768]{1,0:T(8,128)} fusion(bf16[3840,1536]{1,0:T(8,128)(2,1)S(1)} %pad_maximum_fusion, bf16[1024,1280]{1,0:T(8,128)(2,1)S(1)} %get-tuple-element.78, bf16[1024,1280]{1,0:T(8,128)(2,1)S(1)} %copy-done.3, bf16[1024,1280]{1,0:T(8,128)(2,1)S(1)} %get-tuple-element.77), kind=kOutput, calls=%fused_computation.6 | convolution fusion | flops 6063390720 | bytes 16908288 | tf_op jit(solution)/shard_map/dot_general | solution.py:301
  81.9 8.0 %fusion.2 = f32[1024,768]{1,0:T(8,128)S(1)} fusion(bf16[3840,1536]{1,0:T(8,128)(2,1)S(1)} %pad_maximum_fusion, bf16[1024,1280]{1,0:T(8,128)(2,1)S(1)} %get-tuple-element.78, bf16[1024,1280]{1,0:T(8,128)(2,1)} %get-tuple-element.79, bf16[1024,1280]{1,0:T(8,128)(2,1)S(1)} %get-tuple-element.77), kind=kOutput, calls=%fused_computation.8 | convolution fusion | flops 6063390720 | bytes 16908288 | tf_op jit(solution)/shard_map/dot_general | solution.py:300
  89.9 0.1 copy.13.top_ref
  90.0 101.1 %combine.1 = bf16[4,4,4,64,1536]{4,3,2,1,0:T(8,128)(2,1)} custom-call(f32[4,4,64,768]{3,2,1,0:T(8,128)S(1)} %bitcast.90, f32[4,4,64,768]{3,2,1,0:T(8,128)} %bitcast.96, f32[64,1]{1,0:T(8,128)S(1)} %copy.13.top_ref), custom_call_target="tpu_custom_call" | custom-call | tf_op jit(solution)/shard_map/combine/pallas_call | solution.py:235
  191.1 10.5 %copy.23 = bf16[4096,1536]{1,0:T(8,128)(2,1)} copy(bf16[4096,1536]{1,0:T(8,128)(2,1)} %bitcast.91) | data formatting | bytes 25165824
  (12 shorter events, 0.3 us)
Async XLA Ops:
  10.6 1.0 copy-start
  10.6 1.2 copy-start.1
  10.6 1.3 copy-start.2
  72.2 1.7 copy-start.3

commit v3 on v1

v3 whole, which is shorter than its diff:
```python
import functools

import jax
import jax.numpy as jnp
from jax import lax
from jax.experimental import pallas as pl
from jax.experimental.pallas import tpu as pltpu
from jax.sharding import PartitionSpec as P

MESH = pl.DeviceIdType.MESH
SIDE = 4


def split3(a):
    hi = lax.reduce_precision(a, 8, 7)
    rest = a - hi
    mid = lax.reduce_precision(rest, 8, 7)
    low = rest - mid
    return [v.astype(jnp.bfloat16) for v in (hi, mid, low)]


def split3_kernel(a):
    hi = a.astype(jnp.bfloat16)
    rest = a - hi.astype(jnp.float32)
    mid = rest.astype(jnp.bfloat16)
    low = (rest - mid.astype(jnp.float32)).astype(jnp.bfloat16)
    return hi, mid, low


def coords():
    chip = lax.axis_index('etp')
    return chip // (SIDE * SIDE), (chip // SIDE) % SIDE, chip % SIDE


def chip_id(z, y, x):
    return {'etp': ((z % SIDE) * SIDE + y % SIDE) * SIDE + x % SIDE}


def greet(partners):
    barrier = pltpu.get_barrier_semaphore()
    for device_id in partners:
        pl.semaphore_signal(barrier, inc=1, device_id=device_id, device_id_type=MESH)
    pl.semaphore_wait(barrier, len(partners))


def plan(src, dst, sems, n, device_id):
    send_sem, recv_sem = sems
    return pltpu.make_async_remote_copy(src_ref=src, dst_ref=dst, send_sem=send_sem.at[n], recv_sem=recv_sem.at[n],
                                        device_id=device_id, device_id_type=MESH)


def push(src, dst, sems, n, device_id):
    copy = plan(src, dst, sems, n, device_id)
    copy.start()
    return copy


def moe_kernel(hid_hbm, gate_hbm, spread_ref, w_ref, top_ref, out_ref,
               hid, gates, wbuf, part, opp1, fin1, sum1, opp2, fin2, own,
               in_sem, own_sem, ring_send, ring_recv, core_send, core_recv, rs_send, rs_recv, ag_send, ag_recv):
    z, y, x = coords()
    core = lax.axis_index('ep')
    other = {'ep': 1 - core}
    group = (x + y) % SIDE
    n_rows, depth = hid.shape[1:]
    width = part.shape[4]
    rows = w_ref.shape[1] // 2
    cols = 4 * rows
    f32 = jnp.float32
    ups = {'z': chip_id(z + 1, y, x), 'y': chip_id(z, y + 1, x), 'x': chip_id(z, y, x + 1), 'd': chip_id(z, y + 3, x + 1)}
    downs = {'z': chip_id(z + 3, y, x), 'y': chip_id(z, y + 3, x), 'x': chip_id(z, y, x + 3), 'd': chip_id(z, y + 1, x + 3)}

    loads = []
    for zi in range(SIDE):
        for xi in range(SIDE):
            n = zi * SIDE + xi
            chip = zi * SIDE * SIDE + ((group + SIDE - xi) % SIDE) * SIDE + xi
            loads.append(pltpu.make_async_copy(hid_hbm.at[chip], hid.at[n], in_sem.at[n]))
            loads.append(pltpu.make_async_copy(gate_hbm.at[chip], gates.at[n], in_sem.at[16 + n]))
    for load in loads:
        load.start()
    greet(list(ups.values()) + list(downs.values()) + [other])

    rings, cores = (ring_send, ring_recv), (core_send, core_recv)
    cut = (rows * 3 // 5, rows * 2 // 5)

    def span(d, h):
        return pl.ds(0, cut[d]) if h == 0 else pl.ds(cut[d], rows - cut[d])

    def src(d, h):
        start = d * rows + (cut[d] if h else 0)
        return w_ref.at[:, pl.ds(start, rows - cut[d] if h else cut[d]), :]

    def box(q, d, h):
        return wbuf.at[q, :, d, core, span(d, h), :]

    dims = 'xy'
    flights, firsts, seconds, thirds = [], [], [], []
    for d in range(2):
        firsts.append((push(src(d, 0), box(1, d, 0), rings, 6 * d, ups[dims[d]]),
                       push(src(d, 1), box(1, d, 1), rings, 6 * d + 1, downs[dims[d]])))
    owns = []
    for d in range(2):
        owns.append(push(w_ref.at[:, pl.ds(d * rows, rows), :], wbuf.at[0, :, d, core], cores, 7 * d, other))
    for d in range(2):
        seconds.append((push(src(d, 1), box(2, d, 1), rings, 6 * d + 2, ups[dims[d]]),
                        push(src(d, 0), box(2, d, 0), rings, 6 * d + 3, downs[dims[d]])))
    for d in range(2):
        wbuf[0, :, d, core] = w_ref[:, d * rows:(d + 1) * rows, :]
    for load in loads:
        load.wait()
    for copy in owns:
        copy.wait_recv()

    n_half = SIDE * SIDE // 2

    def compute(q, i):
        rows_in = n_half * n_rows
        tokens = hid[pl.ds(n_half * i, n_half)].reshape(rows_in, depth)
        gate = jnp.dot(gates[pl.ds(n_half * i, n_half)].reshape(rows_in, gates.shape[2]), spread_ref[...],
                       preferred_element_type=f32)
        both = lax.dot_general(tokens, wbuf[q, 0:2].reshape(2 * cols, depth), (((1,), (1,)), ((), ())),
                               preferred_element_type=f32)
        h_gate, h_up = both[:, :cols], both[:, cols:]
        act = (jax.nn.silu(h_gate) * h_up).astype(jnp.bfloat16).astype(f32)
        scaled = jnp.where(gate > 0, act * gate, 0.0)
        stack = jnp.concatenate(split3_kernel(scaled), axis=0)
        piece = width // 2
        for n in range(4):
            down = wbuf[q, 2, :, :, :, n * piece:(n + 1) * piece].reshape(cols, piece)
            out = jnp.dot(stack, down, preferred_element_type=f32)
            out = (out[:rows_in] + out[rows_in:2 * rows_in] + out[2 * rows_in:]).reshape(SIDE // 2, SIDE, n_rows, piece)
            where = (n // 2, pl.ds(SIDE // 2 * i, SIDE // 2), slice(None), slice(None), pl.ds((n % 2) * piece, piece))
            part[where] += out

    forwards = [plan(box(1, d, h), box(3, d, h), rings, 6 * d + 4 + h, (ups, downs)[h][dims[d]])
                for d in range(2) for h in range(2)]
    shares = [[plan(box(q, d, h), box(q, d, h), cores, 7 * d + 2 * q - 1 + h, other) for d in range(2) for h in range(2)]
              for q in range(1, SIDE)]
    arrivals = [[copy for pair in firsts for copy in pair], [copy for pair in seconds for copy in pair[::-1]], forwards]

    part[...] = jnp.zeros_like(part)

    @pl.loop(0, 2 * SIDE)
    def _(step):
        for q in range(1, SIDE):
            @pl.when(step == 2 * q - 1)
            def _():
                for n, copy in enumerate(arrivals[q - 1]):
                    copy.wait_recv()
                    if q == 1:
                        forwards[n].start()
                    shares[q - 1][n].start()

            @pl.when(step == 2 * q)
            def _():
                for copy in shares[q - 1]:
                    copy.wait_recv()
        compute(step // 2, step % 2)

    started = arrivals[0] + arrivals[1] + forwards + owns + [copy for share in shares for copy in share]

    sems = (rs_send, rs_recv)
    part_a, part_b = part.at[0], part.at[1]
    def ring_sum(base, ring, me, block, half, opp, fin):
        right, left = ups[ring], downs[ring]
        o, r, l = (me + 2) % SIDE, (me + 1) % SIDE, (me + 3) % SIDE
        one = push(half(block(o), 0), opp.at[0], sems, base, right)
        two = push(half(block(o), 1), opp.at[1], sems, base + 1, left)
        three = push(half(block(r), 1), half(fin.at[0], 1), sems, base + 2, right)
        four = push(half(block(l), 0), half(fin.at[1], 0), sems, base + 3, left)

        def forward():
            one.wait_recv()
            opp[0] = opp[0] + half(block(r), 0)[...]
            five = push(opp.at[0], half(fin.at[0], 0), sems, base + 4, right)
            two.wait_recv()
            opp[1] = opp[1] + half(block(l), 1)[...]
            six = push(opp.at[1], half(fin.at[1], 1), sems, base + 5, left)
            started.extend((one, two, three, four, five, six))

            def finish():
                for copy in (three, four, five, six):
                    copy.wait_recv()
                return block(me)[...] + fin[0] + fin[1]
            return finish
        return forward

    two_blocks = lambda ref, h: ref.at[pl.ds(2 * h, 2)]
    rows_half = lambda ref, h: ref.at[pl.ds(h * (n_rows // 2), n_rows // 2)]
    fwd_a = ring_sum(0, 'z', z, lambda i: part_a.at[i], two_blocks, opp1.at[0], fin1.at[0])
    fwd_b = ring_sum(6, 'd', x, lambda i: part_b.at[:, i], two_blocks, opp1.at[1], fin1.at[1])
    end_a, end_b = fwd_a(), fwd_b()
    sum1[0] = end_a()
    fwd_a = ring_sum(12, 'd', x, lambda i: sum1.at[0, i], rows_half, opp2.at[0], fin2.at[0])
    sum1[1] = end_b()
    fwd_b = ring_sum(18, 'z', z, lambda i: sum1.at[1, i], rows_half, opp2.at[1], fin2.at[1])
    end_a, end_b = fwd_a(), fwd_b()
    mine = jnp.concatenate([end_a(), end_b()], axis=1) * top_ref[...]
    mine = mine.astype(out_ref.dtype)
    own[...] = mine
    keep = pltpu.make_async_copy(own, out_ref.at[z, y, x], own_sem)
    keep.start()

    third = out_ref.shape[4] // 3
    sems_ag = (ag_send, ag_recv)
    where = {'z': z, 'y': y, 'x': x}
    orders = ('xyz', 'yzx', 'zxy')

    def owned(k, h):
        return own.at[pl.ds(h * (n_rows // 2), n_rows // 2), pl.ds(k * third, third)]

    def region(k, done, dim, i, h):
        index = []
        for name in 'zyx':
            if name == dim:
                index.append(i % SIDE)
            elif name in done:
                index.append(slice(None))
            else:
                index.append(where[name])
        return out_ref.at[(*index, pl.ds(h * (n_rows // 2), n_rows // 2), pl.ds(k * third, third))]

    for phase in range(3):
        if phase == 1:
            keep.wait()
        firsts, seconds, thirds = [], [], []
        for k, order in enumerate(orders):
            dim, done = order[phase], order[:phase]
            spot = functools.partial(region, k, done, dim)
            first = functools.partial(owned, k) if phase == 0 else functools.partial(spot, where[dim])
            me, base = where[dim], 18 * phase + 6 * k
            firsts.append((push(first(0), spot(me, 0), sems_ag, base, ups[dim]),
                           push(first(1), spot(me, 1), sems_ag, base + 1, downs[dim])))
        for k, order in enumerate(orders):
            dim, done = order[phase], order[:phase]
            spot = functools.partial(region, k, done, dim)
            first = functools.partial(owned, k) if phase == 0 else functools.partial(spot, where[dim])
            me, base = where[dim], 18 * phase + 6 * k
            seconds.append((push(first(1), spot(me, 1), sems_ag, base + 2, ups[dim]),
                            push(first(0), spot(me, 0), sems_ag, base + 3, downs[dim])))
        for k, order in enumerate(orders):
            dim, done = order[phase], order[:phase]
            spot = functools.partial(region, k, done, dim)
            me, base = where[dim], 18 * phase + 6 * k
            firsts[k][0].wait_recv()
            one = push(spot(me + 3, 0), spot(me + 3, 0), sems_ag, base + 4, ups[dim])
            firsts[k][1].wait_recv()
            two = push(spot(me + 1, 1), spot(me + 1, 1), sems_ag, base + 5, downs[dim])
            thirds.append((one, two))
        for pair in seconds + thirds:
            for copy in pair:
                copy.wait_recv()
        for pair in firsts + seconds + thirds:
            started.extend(pair)
    for copy in started:
        copy.wait_send()


def moe(hid, gates, spread, weights, top):
    blocks, n_rows, depth = hid.shape
    width = depth // 2
    rows = weights.shape[1] // 2
    f32, bf16 = jnp.float32, jnp.bfloat16
    dma = pltpu.SemaphoreType.DMA
    return pl.pallas_call(
        moe_kernel,
        out_shape=jax.ShapeDtypeStruct((SIDE, SIDE, SIDE, n_rows, depth), bf16),
        in_specs=[pl.BlockSpec(memory_space=pl.ANY)] * 2 + [pl.BlockSpec(memory_space=pltpu.VMEM)] * 3,
        out_specs=pl.BlockSpec(memory_space=pl.ANY),
        scratch_shapes=[
            pltpu.VMEM((SIDE * SIDE, n_rows, depth), bf16),
            pltpu.VMEM((SIDE * SIDE, n_rows, gates.shape[2]), bf16),
            pltpu.VMEM((SIDE, 3, 2, 2, rows, depth), bf16),
            pltpu.VMEM((2, SIDE, SIDE, n_rows, width), f32),
            pltpu.VMEM((2, 2, 2, n_rows, width), f32),
            pltpu.VMEM((2, 2, SIDE, n_rows, width), f32),
            pltpu.VMEM((2, SIDE, n_rows, width), f32),
            pltpu.VMEM((2, 2, n_rows // 2, width), f32),
            pltpu.VMEM((2, 2, n_rows, width), f32),
            pltpu.VMEM((n_rows, depth), bf16),
            dma((32,)), dma, dma((12,)), dma((12,)), dma((14,)), dma((14,)), dma((24,)), dma((24,)), dma((54,)), dma((54,)),
        ],
        compiler_params=pltpu.CompilerParams(collective_id=0, has_side_effects=True, vmem_limit_bytes=38 * 2 ** 20),
        name='moe',
    )(hid, gates, spread, weights, top)


def solution(mesh):
    row_spec = P(('dp', 'ep'), None)
    col_spec = P('ep', None, 'etp')
    in_specs = (row_spec, row_spec, row_spec, row_spec, col_spec, col_spec, P('ep', 'etp', None))

    def device_step(hidden, expert_ids, gate_wts, slot_pos, w_gate, w_up, w_down):
        rows, d_model = hidden.shape
        top_k = expert_ids.shape[1]
        local_experts, _, width = w_gate.shape
        experts = 2 * local_experts
        chips = SIDE ** 3
        block = rows // chips

        local = [w.transpose(0, 2, 1) for w in (w_gate, w_up)] + [w_down]
        local = jnp.stack([w.reshape(local_experts * width, d_model) for w in local])

        kept = slot_pos >= 0
        top = jnp.max(jnp.where(kept, gate_wts, 0.0), axis=1, keepdims=True)
        top = jnp.where(top > 0, top, 1.0)
        rel = gate_wts / top
        gate = jnp.zeros((rows, experts), jnp.float32)
        for j in range(top_k):
            hit = (expert_ids[:, j:j + 1] == jnp.arange(experts, dtype=jnp.int32)[None, :]) & kept[:, j:j + 1]
            gate = jnp.where(hit, rel[:, j:j + 1], gate)
        lanes = -(-3 * experts // 128) * 128
        gates = jnp.concatenate(split3(gate) + [jnp.zeros((rows, lanes - 3 * experts), jnp.bfloat16)], axis=1)

        cols = experts * width
        dim, core, expert, _ = jnp.unravel_index(jnp.arange(cols), (2, 2, local_experts // 2, width))
        col_expert = core * local_experts + dim * (local_experts // 2) + expert
        lane = jnp.arange(lanes)[:, None]
        spread = ((lane % experts == col_expert[None, :]) & (lane < 3 * experts)).astype(jnp.bfloat16)
        own_top = lax.dynamic_slice_in_dim(top, lax.axis_index('etp') * block, block, 0)
        out = moe(hidden.reshape(chips, block, d_model), gates.reshape(chips, block, lanes), spread, local, own_top)
        return out.reshape(rows, d_model)

    return jax.shard_map(device_step, mesh=mesh, in_specs=in_specs, out_specs=row_spec, check_vma=False)
```

time: 422 us -> 200 us (0.47)
  waiting for transfers between devices: 341 us -> 0 us
  Pallas kernels: 0 us -> 146 us
  matrix products: 42.3 us -> 0 us
  other arithmetic: 3.8 us -> 44.1 us
  between operations: 13.5 us -> 0.12 us
  blocking collectives: 7.64 us -> 0 us
    reduce_scatter x1 -> x0, waiting for transfers between devices: 252 us -> none  [device_step(): own = lax.psum_scatter(part_sum, 'etp', scatter_dimension=0, tiled=True)]
    pallas_call x0 -> x1, Pallas kernels: none -> 146 us  [moe(): pl.pallas_call(moe_kernel, out_shape=jax.ShapeDtypeStruct((SIDE, SIDE, SI...]
    all_gather x1 -> x0, waiting for transfers between devices: 89.1 us -> none  [device_step(): return lax.all_gather(own, 'etp', axis=0, tiled=True)]
    dot_general x3 -> x0, matrix products: 42.3 us -> none  [the longest x1 20.1 us: device_step(): jnp.dot(parts, jnp.concatenate([wd] * 3, axis=0), preferred_element_type=...]
    convert_element_type x1 -> x4, other arithmetic: 1.76 us -> 40.9 us  [the longest x3 40.8 us: split3(): return [v.astype(jnp.bfloat16) for v in (hi, mid, low)]]
    all_gather x3 -> x0, blocking collectives: 7.64 us -> none  [the longest x1 2.63 us: device_step(): w_down = lax.all_gather(w_down, 'ep', axis=0, tiled=True)]
    unnamed x7 -> x8, local copies, waits for them, and re-layouts: 10.5 us -> 5.14 us
  transfers between devices with their start and end apart: 2 -> 0, of which waited for: 2 -> 0; matrix products, arithmetic and copies ran while one was open for 0% -> 0% of each run, Pallas kernels for 0% -> 0%
where the time goes in v3:
time: 200 us
  Pallas kernels  146 us (73%)
  other arithmetic  44.1 us (22%)
  local copies, waits for them, and re-layouts  9.92 us (5%)
    pallas_call x1, Pallas kernels, moe(): pl.pallas_call(moe_kernel, out_shape=jax.ShapeDtypeStruct((SIDE, SIDE, SI...  146 us
    convert_element_type x3, other arithmetic, split3(): return [v.astype(jnp.bfloat16) for v in (hi, mid, low)]  40.8 us
    unnamed x8, local copies, waits for them, and re-layouts  5.14 us

profile of v3, /device:TPU:0, one launch (start us, length us, event | category | flops | bytes accessed | tf_op | source)
XLA Modules:
  0.0 200.2 jit_solution(11480198981347845478)
XLA Ops:
  0.0 0.1 pad.6.clone
  0.1 1.0 select_reduce_fusion
  1.2 0.1 constant_dynamic-slice_fusion
  1.2 0.4 slice_reduce_fusion.7
  1.6 0.1 and.142
  1.7 0.1 and.163
  1.8 0.1 and.160
  1.8 0.1 and.157
  1.9 0.1 and.154
  2.0 0.1 and.151
  2.1 0.1 and.148
  2.2 0.1 and.145
  2.2 0.1 copy.10
  2.4 0.1 and_convert_fusion.spread_ref
  2.5 0.9 broadcast_divide_fusion
  3.4 0.3 slice_reduce_fusion.15
  3.7 0.1 broadcast_in_dim.97
  3.8 0.1 broadcast_in_dim.111
  3.9 0.1 broadcast_in_dim.109
  4.0 0.1 broadcast_in_dim.107
  4.0 0.1 broadcast_in_dim.105
  4.1 0.1 broadcast_in_dim.103
  4.2 0.1 broadcast_in_dim.101
  4.2 0.1 broadcast_in_dim.99
  4.3 2.2 %slice_reduce_fusion.23 = (s32[4096]{0:T(1024)S(1)}, s32[4096]{0:T(1024)S(1)}, s32[4096]{0:T(1024)S(1)}, s32[4096]{0:T(1024)S(1)}, s32[4096]{0:T(1024)S(1)}, /*i...) fusion(s32[4096,8]{0,1:T(8,128)} %param.12), kind=kLoop, calls=%fused_computation.53 | loop fusion | bytes 262144 | tf_op jit(solution)/shard_map/slice | solution.py:311
  6.5 0.1 eq.162
  6.5 0.1 eq.182
  6.6 0.1 eq.178
  6.7 0.1 eq.174
  6.8 0.1 eq.170
  6.8 0.1 eq.166
  6.9 0.1 eq.190
  7.0 0.1 eq.186
  7.0 13.6 %reduce-precision_convert_fusion = bf16[64,64,40]{2,1,0:T(8,128)(2,1)S(1)} fusion(f32[64,64]{1,0:T(8,128)S(1)} %broadcast_in_dim.111, pred[64,64]{1,0:T(8,128)(4,1)S(1)} %and.163, s32[64,64]{1,0:T(8,128)S(1)} %eq.190, f32[64,64]{1,0:T(8,128)S(1)} %broadcast_in_dim.109, pred[64,64]{1,0:T(8,128)(4,1)S(1)} %and.160, s32[64,64]{1,0:T(8,128)S(1)} %eq.186, ...), kind=kLoop, calls=%fused_computation.1 | loop fusion | flops 4587520 | bytes 622592 | tf_op jit(solution)/shard_map/convert_element_type | solution.py:19
  20.6 13.6 %fusion = bf16[64,64,40]{2,1,0:T(8,128)(2,1)S(1)} fusion(f32[64,64]{1,0:T(8,128)S(1)} %broadcast_in_dim.111, pred[64,64]{1,0:T(8,128)(4,1)S(1)} %and.163, s32[64,64]{1,0:T(8,128)S(1)} %eq.190, f32[64,64]{1,0:T(8,128)S(1)} %broadcast_in_dim.109, pred[64,64]{1,0:T(8,128)(4,1)S(1)} %and.160, s32[64,64]{1,0:T(8,128)S(1)} %eq.186, ...), kind=kLoop, calls=%fused_computation.4 | loop fusion | flops 4751360 | bytes 622592 | tf_op jit(solution)/shard_map/convert_element_type | solution.py:19
  34.3 13.6 %reduce-precision_convert_fusion.1 = bf16[64,64,40]{2,1,0:T(8,128)(2,1)S(1)} fusion(f32[64,64]{1,0:T(8,128)S(1)} %broadcast_in_dim.111, pred[64,64]{1,0:T(8,128)(4,1)S(1)} %and.163, s32[64,64]{1,0:T(8,128)S(1)} %eq.190, f32[64,64]{1,0:T(8,128)S(1)} %broadcast_in_dim.109, pred[64,64]{1,0:T(8,128)(4,1)S(1)} %and.160, s32[64,64]{1,0:T(8,128)S(1)} %eq.186, ...), kind=kLoop, calls=%fused_computation.3 | loop fusion | flops 4259840 | bytes 622592 | tf_op jit(solution)/shard_map/convert_element_type | solution.py:19
  47.8 0.0 copy-start
  47.9 0.0 copy-start.1
  47.9 0.0 copy-start.2
  47.9 1.0 maximum_maximum_fusion.gate_hbm
  48.9 0.0 copy-done
  48.9 0.1 copy-done.1
  49.0 0.1 copy-done.2
  49.2 0.2 pad_maximum_fusion.w_ref
  49.3 146.0 %moe.1 = bf16[4,4,4,64,1536]{4,3,2,1,0:T(8,128)(2,1)S(1)} custom-call(bf16[64,64,1536]{2,1,0:T(8,128)(2,1)} %bitcast.11, bf16[64,64,128]{2,1,0:T(8,128)(2,1)S(1)} %maximum_maximum_fusion.gate_hbm, bf16[128,320]{1,0:T(8,128)(2,1)S(1)} %and_convert_fusion.spread_ref, bf16[3,160,1536]{2,1,0:T(8,128)(2,1)S(1)} %pad_maximum_fusion.w_ref, ...), custom_call_target="tpu_custom_call" | custom-call | tf_op jit(solution)/shard_map/moe/pallas_call | solution.py:266
  195.4 4.8 %copy.12 = bf16[4096,1536]{1,0:T(8,128)(2,1)} copy(bf16[4096,1536]{1,0:T(8,128)(2,1)S(1)} %bitcast.10) | data formatting | bytes 25165824
  (6 shorter events, 0.1 us)
Async XLA Ops:
  47.8 1.1 copy-start
  47.9 1.2 copy-start.1
  47.9 1.3 copy-start.2

commit v4 on v3

--- a/solution.py
+++ b/solution.py
@@ -2,6 +2,7 @@
 
 import jax
 import jax.numpy as jnp
+import numpy as np
 from jax import lax
 from jax.experimental import pallas as pl
 from jax.experimental.pallas import tpu as pltpu
@@ -12,14 +13,6 @@
 
 
 def split3(a):
-    hi = lax.reduce_precision(a, 8, 7)
-    rest = a - hi
-    mid = lax.reduce_precision(rest, 8, 7)
-    low = rest - mid
-    return [v.astype(jnp.bfloat16) for v in (hi, mid, low)]
-
-
-def split3_kernel(a):
     hi = a.astype(jnp.bfloat16)
     rest = a - hi.astype(jnp.float32)
     mid = rest.astype(jnp.bfloat16)
@@ -55,8 +48,8 @@
     return copy
 
 
-def moe_kernel(hid_hbm, gate_hbm, spread_ref, w_ref, top_ref, out_ref,
-               hid, gates, wbuf, part, opp1, fin1, sum1, opp2, fin2, own,
+def moe_kernel(hid_hbm, ids_ref, gate_ref, pos_ref, spread_ref, w_ref, out_ref,
+               hid, terms, gates, wbuf, part, opp1, fin1, sum1, opp2, fin2, own,
                in_sem, own_sem, ring_send, ring_recv, core_send, core_recv, rs_send, rs_recv, ag_send, ag_recv):
     z, y, x = coords()
     core = lax.axis_index('ep')
@@ -76,7 +69,6 @@
             n = zi * SIDE + xi
             chip = zi * SIDE * SIDE + ((group + SIDE - xi) % SIDE) * SIDE + xi
             loads.append(pltpu.make_async_copy(hid_hbm.at[chip], hid.at[n], in_sem.at[n]))
-            loads.append(pltpu.make_async_copy(gate_hbm.at[chip], gates.at[n], in_sem.at[16 + n]))
     for load in loads:
         load.start()
     greet(list(ups.values()) + list(downs.values()) + [other])
@@ -107,6 +99,28 @@
                         push(src(d, 0), box(2, d, 0), rings, 6 * d + 3, downs[dims[d]])))
     for d in range(2):
         wbuf[0, :, d, core] = w_ref[:, d * rows:(d + 1) * rows, :]
+    part[...] = jnp.zeros_like(part)
+
+    kept = pos_ref[...] >= 0
+    top = jnp.max(jnp.where(kept, gate_ref[...], 0.0), axis=0, keepdims=True)
+    top = jnp.where(top > 0, top, 1.0)
+    rel = jnp.where(kept, gate_ref[...] / top, 0.0)
+    ids = ids_ref[...]
+    experts = cols // 8
+    expert = lax.broadcasted_iota(jnp.int32, (experts, ids.shape[1]), 0)
+    dense = jnp.zeros((experts, ids.shape[1]), f32)
+    for j in range(ids.shape[0]):
+        dense = jnp.where(ids[j:j + 1] == expert, rel[j:j + 1], dense)
+    dense = jnp.concatenate([dense, jnp.broadcast_to(top, (8, ids.shape[1]))], axis=0)
+    for n, term in enumerate(split3(dense)):
+        terms[pl.ds(n * (experts + 8), experts + 8)] = term.astype(f32)
+    for zi in range(SIDE):
+        for xi in range(SIDE):
+            tile = zi * 8 + ((group + SIDE - xi) % SIDE) * 2 + xi // 2
+            pair = terms[:, pl.ds(pl.multiple_of(tile * 2 * n_rows, 2 * n_rows), 2 * n_rows)].astype(jnp.bfloat16)
+            spread = lax.dot_general(pair, spread_ref[...], (((0,), (0,)), ((), ())), preferred_element_type=f32)
+            gates[zi * SIDE + xi] = spread[(xi % 2) * n_rows:(xi % 2 + 1) * n_rows]
+
     for load in loads:
         load.wait()
     for copy in owns:
@@ -117,14 +131,13 @@
     def compute(q, i):
         rows_in = n_half * n_rows
         tokens = hid[pl.ds(n_half * i, n_half)].reshape(rows_in, depth)
-        gate = jnp.dot(gates[pl.ds(n_half * i, n_half)].reshape(rows_in, gates.shape[2]), spread_ref[...],
-                       preferred_element_type=f32)
+        gate = gates[pl.ds(n_half * i, n_half)].reshape(rows_in, gates.shape[2])[:, :cols]
         both = lax.dot_general(tokens, wbuf[q, 0:2].reshape(2 * cols, depth), (((1,), (1,)), ((), ())),
                                preferred_element_type=f32)
         h_gate, h_up = both[:, :cols], both[:, cols:]
         act = (jax.nn.silu(h_gate) * h_up).astype(jnp.bfloat16).astype(f32)
         scaled = jnp.where(gate > 0, act * gate, 0.0)
-        stack = jnp.concatenate(split3_kernel(scaled), axis=0)
+        stack = jnp.concatenate(split3(scaled), axis=0)
         piece = width // 2
         for n in range(4):
             down = wbuf[q, 2, :, :, :, n * piece:(n + 1) * piece].reshape(cols, piece)
@@ -138,8 +151,6 @@
     shares = [[plan(box(q, d, h), box(q, d, h), cores, 7 * d + 2 * q - 1 + h, other) for d in range(2) for h in range(2)]
               for q in range(1, SIDE)]
     arrivals = [[copy for pair in firsts for copy in pair], [copy for pair in seconds for copy in pair[::-1]], forwards]
-
-    part[...] = jnp.zeros_like(part)
 
     @pl.loop(0, 2 * SIDE)
     def _(step):
@@ -196,7 +207,7 @@
     sum1[1] = end_b()
     fwd_b = ring_sum(18, 'z', z, lambda i: sum1.at[1, i], rows_half, opp2.at[1], fin2.at[1])
     end_a, end_b = fwd_a(), fwd_b()
-    mine = jnp.concatenate([end_a(), end_b()], axis=1) * top_ref[...]
+    mine = jnp.concatenate([end_a(), end_b()], axis=1) * gates[z * SIDE + x, :, pl.ds(cols, 1)]
     mine = mine.astype(out_ref.dtype)
     own[...] = mine
     keep = pltpu.make_async_copy(own, out_ref.at[z, y, x], own_sem)
@@ -257,7 +268,7 @@
         copy.wait_send()
 
 
-def moe(hid, gates, spread, weights, top):
+def moe(hid, ids, gate_wts, pos, spread, weights):
     blocks, n_rows, depth = hid.shape
     width = depth // 2
     rows = weights.shape[1] // 2
@@ -266,11 +277,12 @@
     return pl.pallas_call(
         moe_kernel,
         out_shape=jax.ShapeDtypeStruct((SIDE, SIDE, SIDE, n_rows, depth), bf16),
-        in_specs=[pl.BlockSpec(memory_space=pl.ANY)] * 2 + [pl.BlockSpec(memory_space=pltpu.VMEM)] * 3,
+        in_specs=[pl.BlockSpec(memory_space=pl.ANY)] + [pl.BlockSpec(memory_space=pltpu.VMEM)] * 5,
         out_specs=pl.BlockSpec(memory_space=pl.ANY),
         scratch_shapes=[
             pltpu.VMEM((SIDE * SIDE, n_rows, depth), bf16),
-            pltpu.VMEM((SIDE * SIDE, n_rows, gates.shape[2]), bf16),
+            pltpu.VMEM((spread.shape[0], ids.shape[1]), f32),
+            pltpu.VMEM((SIDE * SIDE, n_rows, spread.shape[1]), f32),
             pltpu.VMEM((SIDE, 3, 2, 2, rows, depth), bf16),
             pltpu.VMEM((2, SIDE, SIDE, n_rows, width), f32),
             pltpu.VMEM((2, 2, 2, n_rows, width), f32),
@@ -279,11 +291,11 @@
             pltpu.VMEM((2, 2, n_rows // 2, width), f32),
             pltpu.VMEM((2, 2, n_rows, width), f32),
             pltpu.VMEM((n_rows, depth), bf16),
-            dma((32,)), dma, dma((12,)), dma((12,)), dma((14,)), dma((14,)), dma((24,)), dma((24,)), dma((54,)), dma((54,)),
+            dma((16,)), dma, dma((12,)), dma((12,)), dma((14,)), dma((14,)), dma((24,)), dma((24,)), dma((54,)), dma((54,)),
         ],
         compiler_params=pltpu.CompilerParams(collective_id=0, has_side_effects=True, vmem_limit_bytes=38 * 2 ** 20),
         name='moe',
-    )(hid, gates, spread, weights, top)
+    )(hid, ids, gate_wts, pos, spread, weights)
 
 
 def solution(mesh):
@@ -293,7 +305,6 @@
 
     def device_step(hidden, expert_ids, gate_wts, slot_pos, w_gate, w_up, w_down):
         rows, d_model = hidden.shape
-        top_k = expert_ids.shape[1]
         local_experts, _, width = w_gate.shape
         experts = 2 * local_experts
         chips = SIDE ** 3
@@ -302,24 +313,15 @@
         local = [w.transpose(0, 2, 1) for w in (w_gate, w_up)] + [w_down]
         local = jnp.stack([w.reshape(local_experts * width, d_model) for w in local])
 
-        kept = slot_pos >= 0
-        top = jnp.max(jnp.where(kept, gate_wts, 0.0), axis=1, keepdims=True)
-        top = jnp.where(top > 0, top, 1.0)
-        rel = gate_wts / top
-        gate = jnp.zeros((rows, experts), jnp.float32)
-        for j in range(top_k):
-            hit = (expert_ids[:, j:j + 1] == jnp.arange(experts, dtype=jnp.int32)[None, :]) & kept[:, j:j + 1]
-            gate = jnp.where(hit, rel[:, j:j + 1], gate)
-        lanes = -(-3 * experts // 128) * 128
-        gates = jnp.concatenate(split3(gate) + [jnp.zeros((rows, lanes - 3 * experts), jnp.bfloat16)], axis=1)
-
         cols = experts * width
-        dim, core, expert, _ = jnp.unravel_index(jnp.arange(cols), (2, 2, local_experts // 2, width))
-        col_expert = core * local_experts + dim * (local_experts // 2) + expert
-        lane = jnp.arange(lanes)[:, None]
-        spread = ((lane % experts == col_expert[None, :]) & (lane < 3 * experts)).astype(jnp.bfloat16)
-        own_top = lax.dynamic_slice_in_dim(top, lax.axis_index('etp') * block, block, 0)
-        out = moe(hidden.reshape(chips, block, d_model), gates.reshape(chips, block, lanes), spread, local, own_top)
+        per_term = experts + 8
+        dim, core, expert, _ = np.unravel_index(np.arange(cols), (2, 2, local_experts // 2, width))
+        spread = np.zeros((3 * per_term, -(-(cols + 1) // 128) * 128), np.float32)
+        for n in range(3):
+            spread[n * per_term + core * local_experts + dim * (local_experts // 2) + expert, np.arange(cols)] = 1
+            spread[n * per_term + experts, cols] = 1
+        out = moe(hidden.reshape(chips, block, d_model), expert_ids.T, gate_wts.T, slot_pos.T,
+                  jnp.asarray(spread, jnp.bfloat16), local)
         return out.reshape(rows, d_model)
 
     return jax.shard_map(device_step, mesh=mesh, in_specs=in_specs, out_specs=row_spec, check_vma=False)

time: 200 us -> 152 us (0.76)
  other arithmetic: 44.1 us -> 1.54 us
  local copies, waits for them, and re-layouts: 9.92 us -> 4.79 us
    convert_element_type x4 -> x0, other arithmetic: 40.9 us -> none  [the longest x3 40.8 us: split3(): return [v.astype(jnp.bfloat16) for v in (hi, mid, low)]]
    slice x3 -> x0, local copies, waits for them, and re-layouts: 2.85 us -> none  [the longest x1 2.16 us: device_step(): expert_ids[:, j:j + 1] == jnp.arange(experts, dtype=jnp.int32)[None, :]]
    unnamed x8 -> x9, local copies, waits for them, and re-layouts: 5.14 us -> 4.79 us
where the time goes in v4:
time: 152 us
  Pallas kernels  145 us (95%)
  local copies, waits for them, and re-layouts  4.79 us (3%)
  other arithmetic  1.54 us (1%)
    pallas_call x1, Pallas kernels, moe(): pl.pallas_call(moe_kernel, out_shape=jax.ShapeDtypeStruct((SIDE, SIDE, SI...  145 us
    unnamed x9, local copies, waits for them, and re-layouts  4.79 us

profile of v4, /device:TPU:0, one launch (start us, length us, event | category | flops | bytes accessed | tf_op | source)
XLA Modules:
  0.0 151.6 jit_solution(3375355024937501662)
XLA Ops:
  0.0 0.0 copy-start
  0.0 0.0 copy-start.1
  0.0 0.0 copy-start.2
  0.0 0.0 copy-start.3
  0.0 1.5 %pad_maximum_fusion.w_ref = bf16[3,160,1536]{2,1,0:T(8,128)(2,1)S(1)} fusion(bf16[1,160,1536]{2,1,0:T(8,128)(2,1)} %bitcast.17, bf16[1,160,1536]{2,1,0:T(8,128)(2,1)} %bitcast.18, bf16[1,160,1536]{2,1,0:T(8,128)(2,1)} %bitcast.19), kind=kLoop, calls=%fused_computation | loop fusion | flops 1474560 | bytes 2949120 | tf_op jit(solution)/shard_map/stack | solution.py:314
  1.6 0.0 copy-done
  1.6 0.0 copy-done.1
  1.6 0.0 copy-done.2
  1.6 0.0 copy-done.3
  1.6 145.2 %moe.1 = bf16[4,4,4,64,1536]{4,3,2,1,0:T(8,128)(2,1)S(1)} custom-call(bf16[64,64,1536]{2,1,0:T(8,128)(2,1)} %bitcast.16, s32[8,4096]{1,0:T(8,128)S(1)} %bitcast.13, f32[8,4096]{1,0:T(8,128)S(1)} %bitcast.14, s32[8,4096]{1,0:T(8,128)S(1)} %bitcast.15, bf16[144,384]{1,0:T(8,128)(2,1)S(1)} %copy-done.3, bf16[3,160,1536]{2,1,0:T(8,128)(2,1)S(1)} %pad_maximum_fusion.w_ref), custom_call_target="tpu_custom_call" | custom-call | tf_op jit(solution)/shard_map/moe/pallas_call | solution.py:277
  146.9 4.8 %copy.10 = bf16[4096,1536]{1,0:T(8,128)(2,1)} copy(bf16[4096,1536]{1,0:T(8,128)(2,1)S(1)} %bitcast.12) | data formatting | bytes 25165824
Async XLA Ops:
  0.0 1.6 %copy-start = (s32[4096,8]{0,1:T(8,128)S(1)}, s32[4096,8]{0,1:T(8,128)}, u32[]{:S(2)}) copy-start(s32[4096,8]{0,1:T(8,128)} %param.9) | copy-start | bytes 393220
  0.0 1.6 %copy-start.1 = (f32[4096,8]{0,1:T(8,128)S(1)}, f32[4096,8]{0,1:T(8,128)}, u32[]{:S(2)}) copy-start(f32[4096,8]{0,1:T(8,128)} %param.10) | copy-start | bytes 393220
  0.0 1.6 %copy-start.2 = (s32[4096,8]{0,1:T(8,128)S(1)}, s32[4096,8]{0,1:T(8,128)}, u32[]{:S(2)}) copy-start(s32[4096,8]{0,1:T(8,128)} %param.11) | copy-start | bytes 393220
  0.0 1.6 %copy-start.3 = (bf16[144,384]{1,0:T(8,128)(2,1)S(1)}, bf16[144,384]{1,0:T(8,128)(2,1)}, u32[]{:S(2)}) copy-start(bf16[144,384]{1,0:T(8,128)(2,1)} %constant.2.clone.spread_ref) | copy-start | bytes 331780

commit v5 on v4

--- a/solution.py
+++ b/solution.py
@@ -132,19 +132,17 @@
         rows_in = n_half * n_rows
         tokens = hid[pl.ds(n_half * i, n_half)].reshape(rows_in, depth)
         gate = gates[pl.ds(n_half * i, n_half)].reshape(rows_in, gates.shape[2])[:, :cols]
-        both = lax.dot_general(tokens, wbuf[q, 0:2].reshape(2 * cols, depth), (((1,), (1,)), ((), ())),
+        h_gate = lax.dot_general(tokens, wbuf[q, 0].reshape(cols, depth), (((1,), (1,)), ((), ())),
+                                 preferred_element_type=f32)
+        h_up = lax.dot_general(tokens, wbuf[q, 1].reshape(cols, depth), (((1,), (1,)), ((), ())),
                                preferred_element_type=f32)
-        h_gate, h_up = both[:, :cols], both[:, cols:]
         act = (jax.nn.silu(h_gate) * h_up).astype(jnp.bfloat16).astype(f32)
         scaled = jnp.where(gate > 0, act * gate, 0.0)
-        stack = jnp.concatenate(split3(scaled), axis=0)
-        piece = width // 2
-        for n in range(4):
-            down = wbuf[q, 2, :, :, :, n * piece:(n + 1) * piece].reshape(cols, piece)
-            out = jnp.dot(stack, down, preferred_element_type=f32)
-            out = (out[:rows_in] + out[rows_in:2 * rows_in] + out[2 * rows_in:]).reshape(SIDE // 2, SIDE, n_rows, piece)
-            where = (n // 2, pl.ds(SIDE // 2 * i, SIDE // 2), slice(None), slice(None), pl.ds((n % 2) * piece, piece))
-            part[where] += out
+        stack = jnp.concatenate(split3(scaled), axis=1)
+        for n in range(2):
+            down = wbuf[q, 2, :, :, :, n * width:(n + 1) * width].reshape(cols, width)
+            out = jnp.dot(stack, jnp.concatenate([down] * 3, axis=0), preferred_element_type=f32)
+            part[n, pl.ds(SIDE // 2 * i, SIDE // 2)] += out.reshape(SIDE // 2, SIDE, n_rows, width)
 
     forwards = [plan(box(1, d, h), box(3, d, h), rings, 6 * d + 4 + h, (ups, downs)[h][dims[d]])
                 for d in range(2) for h in range(2)]

time: 152 us -> 142 us (0.934)
  Pallas kernels: 145 us -> 135 us
    pallas_call x1, Pallas kernels: 145 us -> 135 us  [moe(): pl.pallas_call(moe_kernel, out_shape=jax.ShapeDtypeStruct((SIDE, SIDE, SI...]
where the time goes in v5:
time: 142 us; the launch traced here: 141 us
  Pallas kernels  135 us (95%)
  local copies, waits for them, and re-layouts  4.79 us (3%)
  other arithmetic  1.54 us (1%)
    pallas_call x1, Pallas kernels, moe(): pl.pallas_call(moe_kernel, out_shape=jax.ShapeDtypeStruct((SIDE, SIDE, SI...  135 us
    unnamed x9, local copies, waits for them, and re-layouts  4.79 us

profile of v5, /device:TPU:0, one launch (start us, length us, event | category | flops | bytes accessed | tf_op | source)
XLA Modules:
  0.0 141.5 jit_solution(16451632021785195552)
XLA Ops:
  0.0 0.0 copy-start
  0.0 0.0 copy-start.1
  0.0 0.0 copy-start.2
  0.0 0.0 copy-start.3
  0.0 1.5 %pad_maximum_fusion.w_ref = bf16[3,160,1536]{2,1,0:T(8,128)(2,1)S(1)} fusion(bf16[1,160,1536]{2,1,0:T(8,128)(2,1)} %bitcast.17, bf16[1,160,1536]{2,1,0:T(8,128)(2,1)} %bitcast.18, bf16[1,160,1536]{2,1,0:T(8,128)(2,1)} %bitcast.19), kind=kLoop, calls=%fused_computation | loop fusion | flops 1474560 | bytes 2949120 | tf_op jit(solution)/shard_map/stack | solution.py:312
  1.6 0.0 copy-done
  1.6 0.0 copy-done.1
  1.6 0.0 copy-done.2
  1.6 0.0 copy-done.3
  1.6 135.1 %moe.1 = bf16[4,4,4,64,1536]{4,3,2,1,0:T(8,128)(2,1)S(1)} custom-call(bf16[64,64,1536]{2,1,0:T(8,128)(2,1)} %bitcast.16, s32[8,4096]{1,0:T(8,128)S(1)} %bitcast.13, f32[8,4096]{1,0:T(8,128)S(1)} %bitcast.14, s32[8,4096]{1,0:T(8,128)S(1)} %bitcast.15, bf16[144,384]{1,0:T(8,128)(2,1)S(1)} %copy-done.3, bf16[3,160,1536]{2,1,0:T(8,128)(2,1)S(1)} %pad_maximum_fusion.w_ref), custom_call_target="tpu_custom_call" | custom-call | tf_op jit(solution)/shard_map/moe/pallas_call | solution.py:275
  136.7 4.8 %copy.10 = bf16[4096,1536]{1,0:T(8,128)(2,1)} copy(bf16[4096,1536]{1,0:T(8,128)(2,1)S(1)} %bitcast.12) | data formatting | bytes 25165824
Async XLA Ops:
  0.0 1.6 %copy-start = (s32[4096,8]{0,1:T(8,128)S(1)}, s32[4096,8]{0,1:T(8,128)}, u32[]{:S(2)}) copy-start(s32[4096,8]{0,1:T(8,128)} %param.9) | copy-start | bytes 393220
  0.0 1.6 %copy-start.1 = (f32[4096,8]{0,1:T(8,128)S(1)}, f32[4096,8]{0,1:T(8,128)}, u32[]{:S(2)}) copy-start(f32[4096,8]{0,1:T(8,128)} %param.10) | copy-start | bytes 393220
  0.0 1.6 %copy-start.2 = (s32[4096,8]{0,1:T(8,128)S(1)}, s32[4096,8]{0,1:T(8,128)}, u32[]{:S(2)}) copy-start(s32[4096,8]{0,1:T(8,128)} %param.11) | copy-start | bytes 393220
  0.0 1.6 %copy-start.3 = (bf16[144,384]{1,0:T(8,128)(2,1)S(1)}, bf16[144,384]{1,0:T(8,128)(2,1)}, u32[]{:S(2)}) copy-start(bf16[144,384]{1,0:T(8,128)(2,1)} %constant.2.clone.spread_ref) | copy-start | bytes 331780

commit v6 on v5

--- a/solution.py
+++ b/solution.py
@@ -10,6 +10,8 @@
 
 MESH = pl.DeviceIdType.MESH
 SIDE = 4
+PLACES = [(2, 2), (2, 1), (1, 2), (2, 3), (3, 2), (2, 0), (0, 2), (1, 1),
+          (3, 1), (1, 3), (3, 3), (0, 1), (1, 0), (0, 3), (3, 0), (0, 0)]
 
 
 def split3(a):
@@ -56,7 +58,7 @@
     other = {'ep': 1 - core}
     group = (x + y) % SIDE
     n_rows, depth = hid.shape[1:]
-    width = part.shape[4]
+    width = part.shape[3]
     rows = w_ref.shape[1] // 2
     cols = 4 * rows
     f32 = jnp.float32
@@ -64,11 +66,12 @@
     downs = {'z': chip_id(z + 3, y, x), 'y': chip_id(z, y + 3, x), 'x': chip_id(z, y, x + 3), 'd': chip_id(z, y + 1, x + 3)}
 
     loads = []
-    for zi in range(SIDE):
-        for xi in range(SIDE):
-            n = zi * SIDE + xi
-            chip = zi * SIDE * SIDE + ((group + SIDE - xi) % SIDE) * SIDE + xi
-            loads.append(pltpu.make_async_copy(hid_hbm.at[chip], hid.at[n], in_sem.at[n]))
+    spots = []
+    for n, (dz, dx) in enumerate(PLACES):
+        zi, xi = (z + dz) % SIDE, (x + dx) % SIDE
+        chip = (zi * SIDE + (group + SIDE - xi) % SIDE) * SIDE + xi
+        spots.append(chip)
+        loads.append(pltpu.make_async_copy(hid_hbm.at[chip], hid.at[n], in_sem.at[n]))
     for load in loads:
         load.start()
     greet(list(ups.values()) + list(downs.values()) + [other])
@@ -114,19 +117,18 @@
     dense = jnp.concatenate([dense, jnp.broadcast_to(top, (8, ids.shape[1]))], axis=0)
     for n, term in enumerate(split3(dense)):
         terms[pl.ds(n * (experts + 8), experts + 8)] = term.astype(f32)
-    for zi in range(SIDE):
-        for xi in range(SIDE):
-            tile = zi * 8 + ((group + SIDE - xi) % SIDE) * 2 + xi // 2
-            pair = terms[:, pl.ds(pl.multiple_of(tile * 2 * n_rows, 2 * n_rows), 2 * n_rows)].astype(jnp.bfloat16)
-            spread = lax.dot_general(pair, spread_ref[...], (((0,), (0,)), ((), ())), preferred_element_type=f32)
-            gates[zi * SIDE + xi] = spread[(xi % 2) * n_rows:(xi % 2 + 1) * n_rows]
+    for n, chip in enumerate(spots):
+        start = pl.multiple_of((chip // 2) * 2 * n_rows, 2 * n_rows)
+        pair = terms[:, pl.ds(start, 2 * n_rows)].astype(jnp.bfloat16)
+        spread = lax.dot_general(pair, spread_ref[...], (((0,), (0,)), ((), ())), preferred_element_type=f32)
+        gates[n] = jnp.where(chip % 2 == 1, spread[n_rows:], spread[:n_rows])
 
     for load in loads:
         load.wait()
     for copy in owns:
         copy.wait_recv()
 
-    n_half = SIDE * SIDE // 2
+    n_half = len(PLACES) // 2
 
     def compute(q, i):
         rows_in = n_half * n_rows
@@ -142,7 +144,7 @@
         for n in range(2):
             down = wbuf[q, 2, :, :, :, n * width:(n + 1) * width].reshape(cols, width)
             out = jnp.dot(stack, jnp.concatenate([down] * 3, axis=0), preferred_element_type=f32)
-            part[n, pl.ds(SIDE // 2 * i, SIDE // 2)] += out.reshape(SIDE // 2, SIDE, n_rows, width)
+            part[n, pl.ds(n_half * i, n_half)] += out.reshape(n_half, n_rows, width)
 
     forwards = [plan(box(1, d, h), box(3, d, h), rings, 6 * d + 4 + h, (ups, downs)[h][dims[d]])
                 for d in range(2) for h in range(2)]
@@ -150,7 +152,7 @@
               for q in range(1, SIDE)]
     arrivals = [[copy for pair in firsts for copy in pair], [copy for pair in seconds for copy in pair[::-1]], forwards]
 
-    @pl.loop(0, 2 * SIDE)
+    @pl.loop(0, 2 * SIDE - 1)
     def _(step):
         for q in range(1, SIDE):
             @pl.when(step == 2 * q - 1)
@@ -170,44 +172,82 @@
     started = arrivals[0] + arrivals[1] + forwards + owns + [copy for share in shares for copy in share]
 
     sems = (rs_send, rs_recv)
-    part_a, part_b = part.at[0], part.at[1]
-    def ring_sum(base, ring, me, block, half, opp, fin):
-        right, left = ups[ring], downs[ring]
-        o, r, l = (me + 2) % SIDE, (me + 1) % SIDE, (me + 3) % SIDE
-        one = push(half(block(o), 0), opp.at[0], sems, base, right)
-        two = push(half(block(o), 1), opp.at[1], sems, base + 1, left)
-        three = push(half(block(r), 1), half(fin.at[0], 1), sems, base + 2, right)
-        four = push(half(block(l), 0), half(fin.at[1], 0), sems, base + 3, left)
-
-        def forward():
-            one.wait_recv()
-            opp[0] = opp[0] + half(block(r), 0)[...]
-            five = push(opp.at[0], half(fin.at[0], 0), sems, base + 4, right)
-            two.wait_recv()
-            opp[1] = opp[1] + half(block(l), 1)[...]
-            six = push(opp.at[1], half(fin.at[1], 1), sems, base + 5, left)
-            started.extend((one, two, three, four, five, six))
-
-            def finish():
-                for copy in (three, four, five, six):
-                    copy.wait_recv()
-                return block(me)[...] + fin[0] + fin[1]
-            return finish
-        return forward
-
-    two_blocks = lambda ref, h: ref.at[pl.ds(2 * h, 2)]
-    rows_half = lambda ref, h: ref.at[pl.ds(h * (n_rows // 2), n_rows // 2)]
-    fwd_a = ring_sum(0, 'z', z, lambda i: part_a.at[i], two_blocks, opp1.at[0], fin1.at[0])
-    fwd_b = ring_sum(6, 'd', x, lambda i: part_b.at[:, i], two_blocks, opp1.at[1], fin1.at[1])
-    end_a, end_b = fwd_a(), fwd_b()
-    sum1[0] = end_a()
-    fwd_a = ring_sum(12, 'd', x, lambda i: sum1.at[0, i], rows_half, opp2.at[0], fin2.at[0])
-    sum1[1] = end_b()
-    fwd_b = ring_sum(18, 'z', z, lambda i: sum1.at[1, i], rows_half, opp2.at[1], fin2.at[1])
-    end_a, end_b = fwd_a(), fwd_b()
-    mine = jnp.concatenate([end_a(), end_b()], axis=1) * gates[z * SIDE + x, :, pl.ds(cols, 1)]
-    mine = mine.astype(out_ref.dtype)
-    own[...] = mine
+    rings_of = ('zd', 'dz')
+    offsets = (2, 1, 3, 0)
+
+    def half(ref, h):
+        return ref.at[pl.ds(h * (n_rows // 2), n_rows // 2)]
+
+    def block(p, i, j):
+        return part.at[p, PLACES.index((i, j) if p == 0 else (j, i))]
+
+    ways = [(ups[r[0]], downs[r[0]]) for r in rings_of]
+    first = [[[plan(half(block(p, 2, j), h), opp1.at[p, h, j], sems, 24 * p + 6 * j + h, ways[p][h])
+               for h in range(2)] for j in range(SIDE)] for p in range(2)]
+    direct = [[[plan(half(block(p, 3 if h else 1, j), 1 - h), half(fin1.at[p, h, j], 1 - h), sems, 24 * p + 6 * j + 2 + h, ways[p][h])
+                for h in range(2)] for j in range(SIDE)] for p in range(2)]
+    onward = [[[plan(opp1.at[p, h, j], half(fin1.at[p, h, j], h), sems, 24 * p + 6 * j + 4 + h, ways[p][h])
+                for h in range(2)] for j in range(SIDE)] for p in range(2)]
+    for group_of in (first, direct, onward):
+        started += [copy for per_part in group_of for pair in per_part for copy in pair]
+
+    def launch(table, k):
+        if k < SIDE:
+            for p in range(2):
+                for copy in table[p][offsets[k]]:
+                    copy.start()
+
+    launch(first, 0)
+    launch(direct, 0)
+    launch(first, 1)
+    compute(SIDE - 1, 1)
+
+    ways2 = [(ups[r[1]], downs[r[1]]) for r in rings_of]
+    first2, direct2 = [[None] * 2 for _ in range(2)], [[None] * 2 for _ in range(2)]
+
+    def finish(k):
+        j = offsets[k]
+        for p in range(2):
+            for h in range(2):
+                direct[p][j][h].wait_recv()
+                onward[p][j][h].wait_recv()
+            sum1[p, j] = block(p, 0, j)[...] + fin1[p, 0, j] + fin1[p, 1, j]
+            base = 48 + 6 * p
+            if j == 2:
+                for h in range(2):
+                    first2[p][h] = push(half(sum1.at[p, j], h), opp2.at[p, h], sems, base + h, ways2[p][h])
+            elif j:
+                h = 0 if j == 1 else 1
+                direct2[p][h] = push(half(sum1.at[p, j], 1 - h), half(fin2.at[p, h], 1 - h), sems, base + 2 + h, ways2[p][h])
+
+    for k in range(SIDE):
+        j = offsets[k]
+        for p in range(2):
+            for h in range(2):
+                first[p][j][h].wait_recv()
+                opp1[p, h, j] = opp1[p, h, j] + half(block(p, 3 if h else 1, j), h)[...]
+                onward[p][j][h].start()
+        launch(direct, k + 1)
+        launch(first, k + 2)
+        if k:
+            finish(k - 1)
+    finish(SIDE - 1)
+    onward2 = [[None] * 2 for _ in range(2)]
+    for p in range(2):
+        for h in range(2):
+            first2[p][h].wait_recv()
+            opp2[p, h] = opp2[p, h] + half(sum1.at[p, 3 if h else 1], h)[...]
+            onward2[p][h] = push(opp2.at[p, h], half(fin2.at[p, h], h), sems, 52 + 6 * p + h, ways2[p][h])
+    total = []
+    for p in range(2):
+        for h in range(2):
+            direct2[p][h].wait_recv()
+            onward2[p][h].wait_recv()
+        total.append(sum1[p, 0] + fin2[p, 0] + fin2[p, 1])
+    for table in (first2, direct2, onward2):
+        started += [copy for pair in table for copy in pair]
+    mine = jnp.concatenate(total, axis=1) * gates[len(PLACES) - 1, :, pl.ds(cols, 1)]
+    own[...] = mine.astype(out_ref.dtype)
     keep = pltpu.make_async_copy(own, out_ref.at[z, y, x], own_sem)
     keep.start()
 
@@ -215,53 +255,71 @@
     sems_ag = (ag_send, ag_recv)
     where = {'z': z, 'y': y, 'x': x}
     orders = ('xyz', 'yzx', 'zxy')
-
-    def owned(k, h):
-        return own.at[pl.ds(h * (n_rows // 2), n_rows // 2), pl.ds(k * third, third)]
-
-    def region(k, done, dim, i, h):
+    shifts = (0, 3, 1, 2)
+    colours = range(3)
+
+    def region(k, phase, s, i, h):
+        order = orders[k]
         index = []
         for name in 'zyx':
-            if name == dim:
-                index.append(i % SIDE)
-            elif name in done:
+            if name == order[phase]:
+                index.append((where[name] + i) % SIDE)
+            elif phase and name == order[phase - 1]:
+                index.append((where[name] + shifts[s]) % SIDE)
+            elif name in order[:phase]:
                 index.append(slice(None))
             else:
                 index.append(where[name])
         return out_ref.at[(*index, pl.ds(h * (n_rows // 2), n_rows // 2), pl.ds(k * third, third))]
 
+    def owned(k, h):
+        return own.at[pl.ds(h * (n_rows // 2), n_rows // 2), pl.ds(k * third, third)]
+
+    def issue(phase, s):
+        copies = []
+        for turn in range(2):
+            for k in colours:
+                dim = orders[k][phase]
+                base = 54 * k + 24 * max(phase - 1, 0) + 6 * (phase > 0) + 6 * s + 2 * turn
+                for way, target in ((0, ups[dim]), (1, downs[dim])):
+                    h = way if turn == 0 else 1 - way
+                    src = owned(k, h) if phase == 0 or (phase == 1 and s == 0) else region(k, phase, s, 0, h)
+                    copies.append((k, turn, way, push(src, region(k, phase, s, 0, h), sems_ag, base + way, target)))
+        started.extend(copy for _, _, _, copy in copies)
+        return {(k, turn, way): copy for k, turn, way, copy in copies}
+
+    def relay(phase, s, sent):
+        passed = {}
+        for k in colours:
+            dim = orders[k][phase]
+            base = 54 * k + 24 * max(phase - 1, 0) + 6 * (phase > 0) + 6 * s + 4
+            for way, target in ((0, ups[dim]), (1, downs[dim])):
+                sent[k, 0, way].wait_recv()
+                spot = region(k, phase, s, 1 if way else 3, way)
+                passed[k, way] = push(spot, spot, sems_ag, base + way, target)
+        started.extend(passed.values())
+        return passed
+
+    def settle(sent_sets, way):
+        for sent in sent_sets:
+            for k in colours:
+                sent[k, 1, way].wait_recv()
+
+    sent = {0: [issue(0, 0)], 1: [issue(1, 0)], 2: []}
     for phase in range(3):
-        if phase == 1:
+        passed = [relay(phase, s, some) for s, some in enumerate(sent[phase])]
+        for way in range(2):
+            settle(sent[phase], way)
+            if phase < 2:
+                sent[phase + 1].append(issue(phase + 1, way + 1))
+        for some in passed:
+            for copy in some.values():
+                copy.wait_recv()
+        if phase < 2:
+            sent[phase + 1].append(issue(phase + 1, 3))
+        if phase == 0:
             keep.wait()
-        firsts, seconds, thirds = [], [], []
-        for k, order in enumerate(orders):
-            dim, done = order[phase], order[:phase]
-            spot = functools.partial(region, k, done, dim)
-            first = functools.partial(owned, k) if phase == 0 else functools.partial(spot, where[dim])
-            me, base = where[dim], 18 * phase + 6 * k
-            firsts.append((push(first(0), spot(me, 0), sems_ag, base, ups[dim]),
-                           push(first(1), spot(me, 1), sems_ag, base + 1, downs[dim])))
-        for k, order in enumerate(orders):
-            dim, done = order[phase], order[:phase]
-            spot = functools.partial(region, k, done, dim)
-            first = functools.partial(owned, k) if phase == 0 else functools.partial(spot, where[dim])
-            me, base = where[dim], 18 * phase + 6 * k
-            seconds.append((push(first(1), spot(me, 1), sems_ag, base + 2, ups[dim]),
-                            push(first(0), spot(me, 0), sems_ag, base + 3, downs[dim])))
-        for k, order in enumerate(orders):
-            dim, done = order[phase], order[:phase]
-            spot = functools.partial(region, k, done, dim)
-            me, base = where[dim], 18 * phase + 6 * k
-            firsts[k][0].wait_recv()
-            one = push(spot(me + 3, 0), spot(me + 3, 0), sems_ag, base + 4, ups[dim])
-            firsts[k][1].wait_recv()
-            two = push(spot(me + 1, 1), spot(me + 1, 1), sems_ag, base + 5, downs[dim])
-            thirds.append((one, two))
-        for pair in seconds + thirds:
-            for copy in pair:
-                copy.wait_recv()
-        for pair in firsts + seconds + thirds:
-            started.extend(pair)
+            sent[2].append(issue(2, 0))
     for copy in started:
         copy.wait_send()
 
@@ -282,14 +340,14 @@
             pltpu.VMEM((spread.shape[0], ids.shape[1]), f32),
             pltpu.VMEM((SIDE * SIDE, n_rows, spread.shape[1]), f32),
             pltpu.VMEM((SIDE, 3, 2, 2, rows, depth), bf16),
-            pltpu.VMEM((2, SIDE, SIDE, n_rows, width), f32),
-            pltpu.VMEM((2, 2, 2, n_rows, width), f32),
+            pltpu.VMEM((2, len(PLACES), n_rows, width), f32),
+            pltpu.VMEM((2, 2, SIDE, n_rows // 2, width), f32),
             pltpu.VMEM((2, 2, SIDE, n_rows, width), f32),
             pltpu.VMEM((2, SIDE, n_rows, width), f32),
             pltpu.VMEM((2, 2, n_rows // 2, width), f32),
             pltpu.VMEM((2, 2, n_rows, width), f32),
             pltpu.VMEM((n_rows, depth), bf16),
-            dma((16,)), dma, dma((12,)), dma((12,)), dma((14,)), dma((14,)), dma((24,)), dma((24,)), dma((54,)), dma((54,)),
+            dma((16,)), dma, dma((12,)), dma((12,)), dma((14,)), dma((14,)), dma((60,)), dma((60,)), dma((162,)), dma((162,)),
         ],
         compiler_params=pltpu.CompilerParams(collective_id=0, has_side_effects=True, vmem_limit_bytes=38 * 2 ** 20),
         name='moe',

time: 142 us -> 137 us (0.965)
  Pallas kernels: 135 us -> 130 us
    pallas_call x1, Pallas kernels: 135 us -> 130 us  [moe(): pl.pallas_call(moe_kernel, out_shape=jax.ShapeDtypeStruct((SIDE, SIDE, SI...]
where the time goes in v6:
time: 137 us; the launch traced here: 136 us
  Pallas kernels  130 us (95%)
  local copies, waits for them, and re-layouts  4.79 us (3%)
  other arithmetic  1.54 us (1%)
    pallas_call x1, Pallas kernels, moe(): pl.pallas_call(moe_kernel, out_shape=jax.ShapeDtypeStruct((SIDE, SIDE, SI...  130 us
    unnamed x9, local copies, waits for them, and re-layouts  4.79 us

profile of v6, /device:TPU:0, one launch (start us, length us, event | category | flops | bytes accessed | tf_op | source)
XLA Modules:
  0.0 136.4 jit_solution(12458492659999221748)
XLA Ops:
  0.0 0.0 copy-start
  0.0 0.0 copy-start.1
  0.0 0.0 copy-start.2
  0.0 0.0 copy-start.3
  0.0 1.5 %pad_maximum_fusion.w_ref = bf16[3,160,1536]{2,1,0:T(8,128)(2,1)S(1)} fusion(bf16[1,160,1536]{2,1,0:T(8,128)(2,1)} %bitcast.17, bf16[1,160,1536]{2,1,0:T(8,128)(2,1)} %bitcast.18, bf16[1,160,1536]{2,1,0:T(8,128)(2,1)} %bitcast.19), kind=kLoop, calls=%fused_computation | loop fusion | flops 1474560 | bytes 2949120 | tf_op jit(solution)/shard_map/stack | solution.py:370
  1.6 0.0 copy-done
  1.6 0.0 copy-done.1
  1.6 0.0 copy-done.2
  1.6 0.0 copy-done.3
  1.6 130.1 %moe.1 = bf16[4,4,4,64,1536]{4,3,2,1,0:T(8,128)(2,1)S(1)} custom-call(bf16[64,64,1536]{2,1,0:T(8,128)(2,1)} %bitcast.16, s32[8,4096]{1,0:T(8,128)S(1)} %bitcast.13, f32[8,4096]{1,0:T(8,128)S(1)} %bitcast.14, s32[8,4096]{1,0:T(8,128)S(1)} %bitcast.15, bf16[144,384]{1,0:T(8,128)(2,1)S(1)} %copy-done.3, bf16[3,160,1536]{2,1,0:T(8,128)(2,1)S(1)} %pad_maximum_fusion.w_ref), custom_call_target="tpu_custom_call" | custom-call | tf_op jit(solution)/shard_map/moe/pallas_call | solution.py:333
  131.7 4.8 %copy.10 = bf16[4096,1536]{1,0:T(8,128)(2,1)} copy(bf16[4096,1536]{1,0:T(8,128)(2,1)S(1)} %bitcast.12) | data formatting | bytes 25165824
Async XLA Ops:
  0.0 1.6 %copy-start = (s32[4096,8]{0,1:T(8,128)S(1)}, s32[4096,8]{0,1:T(8,128)}, u32[]{:S(2)}) copy-start(s32[4096,8]{0,1:T(8,128)} %param.9) | copy-start | bytes 393220
  0.0 1.6 %copy-start.1 = (f32[4096,8]{0,1:T(8,128)S(1)}, f32[4096,8]{0,1:T(8,128)}, u32[]{:S(2)}) copy-start(f32[4096,8]{0,1:T(8,128)} %param.10) | copy-start | bytes 393220
  0.0 1.6 %copy-start.2 = (s32[4096,8]{0,1:T(8,128)S(1)}, s32[4096,8]{0,1:T(8,128)}, u32[]{:S(2)}) copy-start(s32[4096,8]{0,1:T(8,128)} %param.11) | copy-start | bytes 393220
  0.0 1.6 %copy-start.3 = (bf16[144,384]{1,0:T(8,128)(2,1)S(1)}, bf16[144,384]{1,0:T(8,128)(2,1)}, u32[]{:S(2)}) copy-start(bf16[144,384]{1,0:T(8,128)(2,1)} %constant.2.clone.spread_ref) | copy-start | bytes 331780
